TPU v7x, 32 devices: a 4x4x1 block of a 4x4x8 slice. The times are simulated.
32 devices in a mesh: dp: 1 (over z), wy: 4 (over y), wx: 8 (over x, core).
Axes of the slice: x: 4, y: 4, z: 1, core: 2. Of those that a mesh axis runs over, the one named last changes fastest.
The devices are a block of a 4x4x8 slice.
Arguments:
- x_tokens: bfloat16 [32, 128, 2048], P(('dp', 'wy', 'wx'))
- gamma_ln: float32 [2, 2048], replicated
- w_q: bfloat16 [2, 2048, 2048], P(None, 'wx', 'wy')
- w_kv: bfloat16 [2, 2048, 2, 128], P(None, 'wx')
- w_gu: bfloat16 [2, 2048, 2, 8192], P(None, 'wx', None, 'wy')
- w_o: bfloat16 [2, 2048, 2048], P(None, 'wy', 'wx')
- w_d: bfloat16 [2, 8192, 2048], P(None, 'wy', 'wx')
Outputs:
- output 1: bfloat16 [32, 128, 2048], P(('dp', 'wy', 'wx'))
- output 2: bfloat16 [2, 32, 128, 128], P(None, ('dp', 'wy', 'wx'))
- output 3: bfloat16 [2, 32, 128, 128], P(None, ('dp', 'wy', 'wx'))
All inputs are finite; a program needn't handle non-finite values.
Results may differ from a plain program's by a relative error of at most 0.0157459.
Values are sent between devices in bfloat16 or wider.
A program may use at most 768 MiB of HBM per device.

v0:
```python
import jax
import jax.numpy as jnp
from jax import lax
from jax.sharding import PartitionSpec as P

LN_EPS = 1e-6
ROPE_BASE = 10000.0


def rope_tables(seq_len, head_dim):
    half_dim = head_dim // 2
    inv_freq = ROPE_BASE ** (-2.0 * jnp.arange(half_dim, dtype=jnp.float32) / head_dim)
    angles = jnp.arange(seq_len, dtype=jnp.float32)[:, None] * inv_freq[None, :]
    return jnp.cos(angles), jnp.sin(angles)


def rotate(values_in, cos_tab, sin_tab):
    half_dim = values_in.shape[-1] // 2
    first_half = values_in[..., :half_dim].astype(jnp.float32)
    second_half = values_in[..., half_dim:].astype(jnp.float32)
    rotated = jnp.concatenate([first_half * cos_tab - second_half * sin_tab, second_half * cos_tab + first_half * sin_tab], axis=-1)
    return rotated.astype(jnp.bfloat16)


def layer_norm(resid, g_scale):
    resid_f = resid.astype(jnp.float32)
    centered = resid_f - jnp.mean(resid_f, axis=-1, keepdims=True)
    variance = jnp.mean(centered * centered, axis=-1, keepdims=True)
    return (centered * lax.rsqrt(variance + LN_EPS) * g_scale).astype(jnp.bfloat16)


def causal_attention(q_rot, k_rot, v_val):
    seq_len = q_rot.shape[1]
    score_scale = q_rot.shape[-1] ** -0.5
    scores = jnp.einsum('bshe,bte->bhst', q_rot, k_rot, preferred_element_type=jnp.float32) * score_scale
    allowed = jnp.arange(seq_len)[:, None] >= jnp.arange(seq_len)[None, :]
    scores = jnp.where(allowed, scores, -jnp.inf)
    attn_probs = jax.nn.softmax(scores, axis=-1).astype(jnp.bfloat16)
    attended = jnp.einsum('bhst,bte->bshe', attn_probs, v_val, preferred_element_type=jnp.float32)
    return attended.astype(jnp.bfloat16)


def decoder_layer(resid, g_scale, w_q, w_kv, w_gu, w_o, w_d, cos_tab, sin_tab):
    batch_loc, seq_len = resid.shape[0], resid.shape[1]
    head_dim = w_kv.shape[-1]
    normed = layer_norm(resid, g_scale)
    q_proj = jnp.einsum('bsd,dn->bsn', normed, w_q, preferred_element_type=jnp.float32).astype(jnp.bfloat16)
    kv_proj = jnp.einsum('bsd,dce->bsce', normed, w_kv, preferred_element_type=jnp.float32).astype(jnp.bfloat16)
    gu_proj = jnp.einsum('bsd,dcf->bscf', normed, w_gu, preferred_element_type=jnp.float32).astype(jnp.bfloat16)
    q_rot = rotate(q_proj.reshape(batch_loc, seq_len, -1, head_dim), cos_tab[:, None, :], sin_tab[:, None, :])
    k_rot = rotate(kv_proj[:, :, 0], cos_tab, sin_tab)
    v_val = kv_proj[:, :, 1]
    attended = causal_attention(q_rot, k_rot, v_val).reshape(batch_loc, seq_len, -1)
    hidden = (jax.nn.silu(gu_proj[:, :, 0].astype(jnp.float32)) * gu_proj[:, :, 1].astype(jnp.float32)).astype(jnp.bfloat16)
    mixed = jnp.einsum('bsn,nd->bsd', attended, w_o, preferred_element_type=jnp.float32) + jnp.einsum('bsf,fd->bsd', hidden, w_d, preferred_element_type=jnp.float32)
    return (resid.astype(jnp.float32) + mixed).astype(jnp.bfloat16), k_rot, v_val


def solution(mesh):
    batch_axes = ('dp', 'wy', 'wx')
    in_specs = (P(batch_axes), P(), P(None, 'wx', 'wy'), P(None, 'wx'), P(None, 'wx', None, 'wy'), P(None, 'wy', 'wx'), P(None, 'wy', 'wx'))
    out_specs = (P(batch_axes), P(None, batch_axes), P(None, batch_axes))

    def device_step(x_tokens, gamma_ln, w_q, w_kv, w_gu, w_o, w_d):
        cos_tab, sin_tab = rope_tables(x_tokens.shape[1], w_kv.shape[-1])
        resid = x_tokens
        key_list = []
        value_list = []
        for layer_idx in range(w_q.shape[0]):
            full_q = lax.all_gather(lax.all_gather(w_q[layer_idx], 'wy', axis=1, tiled=True), 'wx', axis=0, tiled=True)
            full_kv = lax.all_gather(w_kv[layer_idx], 'wx', axis=0, tiled=True)
            full_gu = lax.all_gather(lax.all_gather(w_gu[layer_idx], 'wy', axis=2, tiled=True), 'wx', axis=0, tiled=True)
            full_o = lax.all_gather(lax.all_gather(w_o[layer_idx], 'wy', axis=0, tiled=True), 'wx', axis=1, tiled=True)
            full_d = lax.all_gather(lax.all_gather(w_d[layer_idx], 'wy', axis=0, tiled=True), 'wx', axis=1, tiled=True)
            resid, k_rot, v_val = decoder_layer(resid, gamma_ln[layer_idx], full_q, full_kv, full_gu, full_o, full_d, cos_tab, sin_tab)
            key_list.append(k_rot)
            value_list.append(v_val)
        return resid, jnp.stack(key_list), jnp.stack(value_list)

    return jax.shard_map(device_step, mesh=mesh, in_specs=in_specs, out_specs=out_specs, check_vma=False)
```

profile of v0, /device:TPU:97, one launch (start us, length us, event | category | flops | bytes accessed | tf_op | source)
XLA Modules:
  0.0 1560.1 jit_solution(6537362027086705515)
XLA Ops:
  7.2 1.9 fusion.148
  9.3 1.9 fusion.146
  11.3 4.7 fusion.144
  16.0 2.2 copy.46
  18.3 3.0 fusion.145
  21.5 0.6 all-gather.57.cloned.1.call-update
  22.1 0.6 all-gather.61.cloned.1.call-update
  22.8 2.2 copy.50
  25.1 0.7 all-gather.69.cloned.1.call-update
  26.1 0.8 copy.43
  27.0 5.8 all-gather.39.cloned.1.call-done
  32.9 23.3 %all-gather.43.cloned.1.call-done = bf16[1,2048,256]{2,1,0:T(8,128)(2,1)} async-done(((bf16[1,512,256]{2,1,0:T(8,128)(2,1)}), bf16[1,2048,256]{2,1,0:T(8,128)(2,1)}) %all-gather.43.cloned.1.call-update) | async-done | bytes 1048592 | tf_op jit(solution)/shard_map/all_gather | solution.py:73
  56.3 84.7 %all-gather.47.cloned.1.call-done = bf16[1,256,2,8192]{3,1,2,0:T(8,128)(2,1)} async-done(((bf16[1,256,2,2048]{3,1,2,0:T(8,128)(2,1)}), bf16[1,256,2,8192]{3,1,2,0:T(8,128)(2,1)}) %all-gather.47.cloned.1.call-update) | async-done | bytes 8388624 | tf_op jit(solution)/shard_map/all_gather | solution.py:72
  141.1 47.8 %all-gather.51.cloned.1.call-done = bf16[1,8192,256]{2,1,0:T(8,128)(2,1)} async-done(((bf16[1,2048,256]{2,1,0:T(8,128)(2,1)}), bf16[1,8192,256]{2,1,0:T(8,128)(2,1)}) %all-gather.51.cloned.1.call-update) | async-done | bytes 4194320 | tf_op jit(solution)/shard_map/all_gather | solution.py:74
  189.0 0.8 copy.47
  189.9 20.8 %all-gather.57.cloned.1.call-done = bf16[1,256,2048]{2,1,0:T(8,128)(2,1)} async-done(((bf16[1,256,512]{2,1,0:T(8,128)(2,1)}), bf16[1,256,2048]{2,1,0:T(8,128)(2,1)}) %all-gather.57.cloned.1.call-update) | async-done | bytes 1048592 | tf_op jit(solution)/shard_map/all_gather | solution.py:70
  210.8 23.2 %all-gather.61.cloned.1.call-done = bf16[1,2048,256]{2,1,0:T(8,128)(2,1)} async-done(((bf16[1,512,256]{2,1,0:T(8,128)(2,1)}), bf16[1,2048,256]{2,1,0:T(8,128)(2,1)}) %all-gather.61.cloned.1.call-update) | async-done | bytes 1048592 | tf_op jit(solution)/shard_map/all_gather | solution.py:73
  234.1 84.7 %all-gather.65.cloned.1.call-done = bf16[1,256,2,8192]{3,1,2,0:T(8,128)(2,1)} async-done(((bf16[1,256,2,2048]{3,1,2,0:T(8,128)(2,1)}), bf16[1,256,2,8192]{3,1,2,0:T(8,128)(2,1)}) %all-gather.65.cloned.1.call-update) | async-done | bytes 8388624 | tf_op jit(solution)/shard_map/all_gather | solution.py:72
  318.9 47.9 %all-gather.69.cloned.1.call-done = bf16[1,8192,256]{2,1,0:T(8,128)(2,1)} async-done(((bf16[1,2048,256]{2,1,0:T(8,128)(2,1)}), bf16[1,8192,256]{2,1,0:T(8,128)(2,1)}) %all-gather.69.cloned.1.call-update) | async-done | bytes 4194320 | tf_op jit(solution)/shard_map/all_gather | solution.py:74
  367.1 0.3 fusion.84
  367.7 22.3 %all-gather.37.cloned.1.call-done = bf16[1,2048,2,128]{1,3,2,0:T(8,128)(2,1)} async-done(((bf16[1,256,2,128]{1,3,2,0:T(8,128)(2,1)}), bf16[1,2048,2,128]{1,3,2,0:T(8,128)(2,1)}) %all-gather.37.cloned.1.call-update) | async-done | bytes 1048592 | tf_op jit(solution)/shard_map/all_gather | solution.py:71
  390.0 1.8 fusion.115
  392.0 47.4 %all-gather.41.cloned.1.call-done = bf16[1,2048,2048]{2,1,0:T(8,128)(2,1)} async-done(((bf16[1,256,2048]{2,1,0:T(8,128)(2,1)}), bf16[1,2048,2048]{2,1,0:T(8,128)(2,1)}) %all-gather.41.cloned.1.call-update) | async-done | bytes 8388624 | tf_op jit(solution)/shard_map/all_gather | solution.py:70
  439.4 4.7 fusion.81
  444.4 0.4 fusion.100
  444.8 0.5 fusion.152
  445.5 0.3 convolution_convert_fusion.1
  445.8 45.7 %all-gather.45.cloned.1.call-done = bf16[1,2048,2048]{2,1,0:T(8,128)(2,1)} async-done(((bf16[1,2048,256]{2,1,0:T(8,128)(2,1)}), bf16[1,2048,2048]{2,1,0:T(8,128)(2,1)}) %all-gather.45.cloned.1.call-update) | async-done | bytes 8388624 | tf_op jit(solution)/shard_map/all_gather | solution.py:73
  491.6 4.7 fusion.24
  496.2 292.5 %all-gather.49.cloned.1.call-done = bf16[1,2048,2,8192]{3,1,2,0:T(8,128)(2,1)} async-done(((bf16[1,256,2,8192]{3,1,2,0:T(8,128)(2,1)}), bf16[1,2048,2,8192]{3,1,2,0:T(8,128)(2,1)}) %all-gather.49.cloned.1.call-update) | async-done | bytes 67108880 | tf_op jit(solution)/shard_map/all_gather | solution.py:72
  788.8 25.5 %fusion.17 = bf16[1,128,2,8192]{3,1,2,0:T(8,128)(2,1)} fusion(bf16[1,2048,2,8192]{3,1,2,0:T(8,128)(2,1)} %all-gather.49.cloned.1.call-done, bf16[1,128,2048]{2,1,0:T(8,128)(2,1)S(1)} %copy-done, f32[2048]{0:T(1024)S(1)} %bitcast.222, f32[128]{0:T(128)S(1)} %add_rsqrt_fusion.1, f32[128]{0:T(128)S(1)} %broadcast_multiply_fusion.1), kind=kOutput, calls=%fused_computation.11 | convolution fusion | flops 8593342464 | bytes 71836672 | tf_op jit(solution)/shard_map/bsd,dcf->bscf/dot_general | solution.py:49
  814.3 137.2 %all-gather.53.cloned.1.call-done = bf16[1,8192,2048]{2,1,0:T(8,128)(2,1)} async-done(((bf16[1,8192,256]{2,1,0:T(8,128)(2,1)}), bf16[1,8192,2048]{2,1,0:T(8,128)(2,1)}) %all-gather.53.cloned.1.call-update) | async-done | bytes 33554448 | tf_op jit(solution)/shard_map/all_gather | solution.py:74
  951.5 14.7 fusion.153
  966.7 7.8 all-gather.55.cloned.1.call-done
  974.5 1.7 fusion.110
  976.4 0.7 copy.35
  977.1 46.7 %all-gather.59.cloned.1.call-done = bf16[1,2048,2048]{2,1,0:T(8,128)(2,1)} async-done(((bf16[1,256,2048]{2,1,0:T(8,128)(2,1)}), bf16[1,2048,2048]{2,1,0:T(8,128)(2,1)}) %all-gather.59.cloned.1.call-update) | async-done | bytes 8388624 | tf_op jit(solution)/shard_map/all_gather | solution.py:70
  1023.8 4.6 fusion.59
  1029.4 0.7 copy.36
  1030.1 0.4 fusion.98
  1030.5 0.5 fusion.154
  1031.2 0.3 convolution_convert_fusion
  1031.5 44.4 %all-gather.63.cloned.1.call-done = bf16[1,2048,2048]{2,1,0:T(8,128)(2,1)} async-done(((bf16[1,2048,256]{2,1,0:T(8,128)(2,1)}), bf16[1,2048,2048]{2,1,0:T(8,128)(2,1)}) %all-gather.63.cloned.1.call-update) | async-done | bytes 8388624 | tf_op jit(solution)/shard_map/all_gather | solution.py:73
  1075.9 4.7 fusion.20
  1080.5 292.5 %all-gather.67.cloned.1.call-done = bf16[1,2048,2,8192]{3,1,2,0:T(8,128)(2,1)} async-done(((bf16[1,256,2,8192]{3,1,2,0:T(8,128)(2,1)}), bf16[1,2048,2,8192]{3,1,2,0:T(8,128)(2,1)}) %all-gather.67.cloned.1.call-update) | async-done | bytes 67108880 | tf_op jit(solution)/shard_map/all_gather | solution.py:72
  1373.0 25.3 %fusion.14 = bf16[1,128,2,8192]{3,1,2,0:T(8,128)(2,1)} fusion(bf16[1,2048,2,8192]{3,1,2,0:T(8,128)(2,1)} %all-gather.67.cloned.1.call-done, bf16[1,128,2048]{2,1,0:T(8,128)(2,1)S(1)} %multiply_convert_fusion), kind=kOutput, calls=%fused_computation.10 | convolution fusion | flops 8592031744 | bytes 71827456 | tf_op jit(solution)/shard_map/bsd,dcf->bscf/dot_general | solution.py:49
  1398.3 137.3 %all-gather.71.cloned.1.call-done = bf16[1,8192,2048]{2,1,0:T(8,128)(2,1)} async-done(((bf16[1,8192,256]{2,1,0:T(8,128)(2,1)}), bf16[1,8192,2048]{2,1,0:T(8,128)(2,1)}) %all-gather.71.cloned.1.call-update) | async-done | bytes 33554448 | tf_op jit(solution)/shard_map/all_gather | solution.py:74
  1535.6 17.6 %fusion.62 = bf16[1,128,2048]{2,1,0:T(8,128)(2,1)} fusion(f32[1,128,2048]{2,1,0:T(8,128)S(1)} %get-tuple-element.42, f32[128,2048]{1,0:T(8,128)S(1)} %fusion.20, bf16[1,8192,2048]{2,1,0:T(8,128)(2,1)} %all-gather.71.cloned.1.call-done, bf16[1,128,2,8192]{3,1,2,0:T(8,128)(2,1)} %fusion.14), kind=kOutput, calls=%fused_computation.42 | convolution fusion | flops 4304142336 | bytes 40370176 | tf_op jit(solution)/shard_map/bsf,fd->bsd/dot_general | solution.py:55
  (67 shorter events, 5.1 us)
Async XLA Ops:
  7.2 25.6 %all-gather.39.cloned.1.call-start = ((), (), s32[]{:S(2)}) async-start(), calls=%async_computation.1 | async-start | bytes 1310720 | tf_op jit(solution)/shard_map/all_gather | solution.py:70
  9.2 47.0 %all-gather.43.cloned.1.call-start = ((), (), s32[]{:S(2)}) async-start(), calls=%async_computation.3 | async-start | bytes 1310720 | tf_op jit(solution)/shard_map/all_gather | solution.py:73
  11.2 129.8 %all-gather.47.cloned.1.call-start = ((), (), s32[]{:S(2)}) async-start(), calls=%async_computation.5 | async-start | bytes 10485760 | tf_op jit(solution)/shard_map/all_gather | solution.py:72
  18.3 170.6 %all-gather.51.cloned.1.call-start = ((), (), s32[]{:S(2)}) async-start(), calls=%async_computation.7 | async-start | bytes 5242880 | tf_op jit(solution)/shard_map/all_gather | solution.py:74
  21.4 4.5 copy-start.1
  21.4 189.3 %all-gather.57.cloned.1.call-start = ((), (), s32[]{:S(2)}) async-start(), calls=%async_computation.10 | async-start | bytes 1310720 | tf_op jit(solution)/shard_map/all_gather | solution.py:70
  22.1 211.9 %all-gather.61.cloned.1.call-start = ((), (), s32[]{:S(2)}) async-start(), calls=%async_computation.12 | async-start | bytes 1310720 | tf_op jit(solution)/shard_map/all_gather | solution.py:73
  22.7 296.1 %all-gather.65.cloned.1.call-start = ((), (), s32[]{:S(2)}) async-start(), calls=%async_computation.14 | async-start | bytes 10485760 | tf_op jit(solution)/shard_map/all_gather | solution.py:72
  25.0 341.8 %all-gather.69.cloned.1.call-start = ((), (), s32[]{:S(2)}) async-start(), calls=%async_computation.16 | async-start | bytes 5242880 | tf_op jit(solution)/shard_map/all_gather | solution.py:74
  25.9 364.1 %all-gather.37.cloned.1.call-start = ((), (), s32[]{:S(2)}) async-start(), calls=%async_computation | async-start | bytes 1179648 | tf_op jit(solution)/shard_map/all_gather | solution.py:71
  26.9 412.4 %all-gather.41.cloned.1.call-start = ((), (), s32[]{:S(2)}) async-start(), calls=%async_computation.2 | async-start | bytes 9437184 | tf_op jit(solution)/shard_map/all_gather | solution.py:70
  32.8 458.7 %all-gather.45.cloned.1.call-start = ((), (), s32[]{:S(2)}) async-start(), calls=%async_computation.4 | async-start | bytes 9437184 | tf_op jit(solution)/shard_map/all_gather | solution.py:73
  56.2 732.5 %all-gather.49.cloned.1.call-start = ((), (), s32[]{:S(2)}) async-start(), calls=%async_computation.6 | async-start | bytes 75497472 | tf_op jit(solution)/shard_map/all_gather | solution.py:72
  141.0 810.4 %all-gather.53.cloned.1.call-start = ((), (), s32[]{:S(2)}) async-start(), calls=%async_computation.8 | async-start | bytes 37748736 | tf_op jit(solution)/shard_map/all_gather | solution.py:74
  188.9 785.6 %all-gather.55.cloned.1.call-start = ((), (), s32[]{:S(2)}) async-start(), calls=%async_computation.9 | async-start | bytes 1179648 | tf_op jit(solution)/shard_map/all_gather | solution.py:71
  189.8 834.0 %all-gather.59.cloned.1.call-start = ((), (), s32[]{:S(2)}) async-start(), calls=%async_computation.11 | async-start | bytes 9437184 | tf_op jit(solution)/shard_map/all_gather | solution.py:70
  210.8 865.1 %all-gather.63.cloned.1.call-start = ((), (), s32[]{:S(2)}) async-start(), calls=%async_computation.13 | async-start | bytes 9437184 | tf_op jit(solution)/shard_map/all_gather | solution.py:73
  234.0 1139.0 %all-gather.67.cloned.1.call-start = ((), (), s32[]{:S(2)}) async-start(), calls=%async_computation.15 | async-start | bytes 75497472 | tf_op jit(solution)/shard_map/all_gather | solution.py:72
  318.9 48.1 %copy-start = (bf16[1,128,2048]{2,1,0:T(8,128)(2,1)S(1)}, bf16[1,128,2048]{2,1,0:T(8,128)(2,1)}, u32[]{:S(2)}) copy-start(bf16[1,128,2048]{2,1,0:T(8,128)(2,1)} %param.7) | copy-start | bytes 1572868
  318.9 48.8 %copy-start.2 = (f32[2,2048]{1,0:T(2,128)S(1)}, f32[2,2048]{1,0:T(2,128)}, u32[]{:S(2)}) copy-start(f32[2,2048]{1,0:T(2,128)} %param.8) | copy-start | bytes 49156
  318.9 1216.8 %all-gather.71.cloned.1.call-start = ((), (), s32[]{:S(2)}) async-start(), calls=%async_computation.17 | async-start | bytes 37748736 | tf_op jit(solution)/shard_map/all_gather | solution.py:74
Sparse Core Ops, SparseCore 0:
  9.6 23.1 all-gather.38
  34.3 21.7 all-gather.42
  57.7 83.2 all-gather.46
  142.4 46.4 all-gather.50
  190.9 19.7 all-gather.56
  212.1 21.8 all-gather.60
  235.5 83.2 all-gather.64
  320.4 46.4 all-gather.68
  368.4 21.5 all-gather.36
  391.5 47.8 all-gather.40
  441.0 50.5 all-gather.44
  493.0 295.6 all-gather.48
  790.3 161.1 all-gather.52
  952.9 21.5 all-gather.54
  975.9 47.8 all-gather.58
  1025.3 50.5 all-gather.62
  1077.3 295.6 all-gather.66
  1374.5 161.1 all-gather.70
where the time goes:
time: 1560 us
  waiting for transfers between devices  1410 us (90%)
  matrix products  107 us (7%)
  local copies, waits for them, and re-layouts  20.3 us (1%)
    all_gather x2, waiting for transfers between devices, device_step(): lax.all_gather(lax.all_gather(w_gu[layer_idx], 'wy', axis=2, tiled=True),...  585 us
    all_gather x2, waiting for transfers between devices, device_step(): lax.all_gather(lax.all_gather(w_d[layer_idx], 'wy', axis=0, tiled=True),...  275 us
    all_gather x2, waiting for transfers between devices, device_step(): lax.all_gather(w_gu[layer_idx], 'wy', axis=2, tiled=True)  169 us
    all_gather x2, waiting for transfers between devices, device_step(): lax.all_gather(w_d[layer_idx], 'wy', axis=0, tiled=True)  95.6 us
    all_gather x2, waiting for transfers between devices, device_step(): lax.all_gather(lax.all_gather(w_q[layer_idx], 'wy', axis=1, tiled=True),...  94.1 us
    all_gather x2, waiting for transfers between devices, device_step(): lax.all_gather(lax.all_gather(w_o[layer_idx], 'wy', axis=0, tiled=True),...  90.1 us
    dot_general x2, matrix products, decoder_layer(): jnp.einsum('bsd,dcf->bscf', normed, w_gu, preferred_element_type=jnp.floa...  50.8 us
    all_gather x2, waiting for transfers between devices, device_step(): lax.all_gather(w_o[layer_idx], 'wy', axis=0, tiled=True)  46.4 us
  transfers between devices with their start and end apart: 18, of which 18 were waited for; matrix products, arithmetic and copies ran while one was open for 7% of the time, Pallas kernels for 0%

commit v1 on v0

--- a/solution.py
+++ b/solution.py
@@ -41,19 +41,25 @@
 
 
 def decoder_layer(resid, g_scale, w_q, w_kv, w_gu, w_o, w_d, cos_tab, sin_tab):
-    batch_loc, seq_len = resid.shape[0], resid.shape[1]
     head_dim = w_kv.shape[-1]
     normed = layer_norm(resid, g_scale)
-    q_proj = jnp.einsum('bsd,dn->bsn', normed, w_q, preferred_element_type=jnp.float32).astype(jnp.bfloat16)
-    kv_proj = jnp.einsum('bsd,dce->bsce', normed, w_kv, preferred_element_type=jnp.float32).astype(jnp.bfloat16)
-    gu_proj = jnp.einsum('bsd,dcf->bscf', normed, w_gu, preferred_element_type=jnp.float32).astype(jnp.bfloat16)
-    q_rot = rotate(q_proj.reshape(batch_loc, seq_len, -1, head_dim), cos_tab[:, None, :], sin_tab[:, None, :])
+    group = lax.all_gather(normed, 'wy', axis=0, tiled=True)
+    batch_grp, seq_len = group.shape[0], group.shape[1]
+    q_proj = jnp.einsum('bsd,dn->bsn', group, w_q, preferred_element_type=jnp.float32).astype(jnp.bfloat16)
+    kv_proj = jnp.einsum('bsd,dce->bsce', group, w_kv, preferred_element_type=jnp.float32).astype(jnp.bfloat16)
+    gu_proj = jnp.einsum('bsd,dcf->bscf', group, w_gu, preferred_element_type=jnp.float32).astype(jnp.bfloat16)
+    q_rot = rotate(q_proj.reshape(batch_grp, seq_len, -1, head_dim), cos_tab[:, None, :], sin_tab[:, None, :])
     k_rot = rotate(kv_proj[:, :, 0], cos_tab, sin_tab)
     v_val = kv_proj[:, :, 1]
-    attended = causal_attention(q_rot, k_rot, v_val).reshape(batch_loc, seq_len, -1)
+    attended = causal_attention(q_rot, k_rot, v_val).reshape(batch_grp, seq_len, -1)
     hidden = (jax.nn.silu(gu_proj[:, :, 0].astype(jnp.float32)) * gu_proj[:, :, 1].astype(jnp.float32)).astype(jnp.bfloat16)
-    mixed = jnp.einsum('bsn,nd->bsd', attended, w_o, preferred_element_type=jnp.float32) + jnp.einsum('bsf,fd->bsd', hidden, w_d, preferred_element_type=jnp.float32)
-    return (resid.astype(jnp.float32) + mixed).astype(jnp.bfloat16), k_rot, v_val
+    partial = jnp.einsum('bsn,nd->bsd', attended, w_o, preferred_element_type=jnp.float32) + jnp.einsum('bsf,fd->bsd', hidden, w_d, preferred_element_type=jnp.float32)
+    mixed = lax.psum_scatter(partial, 'wy', scatter_dimension=0, tiled=True)
+    batch_loc = resid.shape[0]
+    mine = lax.axis_index('wy') * batch_loc
+    k_own = lax.dynamic_slice_in_dim(k_rot, mine, batch_loc, 0)
+    v_own = lax.dynamic_slice_in_dim(v_val, mine, batch_loc, 0)
+    return (resid.astype(jnp.float32) + mixed).astype(jnp.bfloat16), k_own, v_own
 
 
 def solution(mesh):
@@ -67,11 +73,11 @@
         key_list = []
         value_list = []
         for layer_idx in range(w_q.shape[0]):
-            full_q = lax.all_gather(lax.all_gather(w_q[layer_idx], 'wy', axis=1, tiled=True), 'wx', axis=0, tiled=True)
+            full_q = lax.all_gather(w_q[layer_idx], 'wx', axis=0, tiled=True)
             full_kv = lax.all_gather(w_kv[layer_idx], 'wx', axis=0, tiled=True)
-            full_gu = lax.all_gather(lax.all_gather(w_gu[layer_idx], 'wy', axis=2, tiled=True), 'wx', axis=0, tiled=True)
-            full_o = lax.all_gather(lax.all_gather(w_o[layer_idx], 'wy', axis=0, tiled=True), 'wx', axis=1, tiled=True)
-            full_d = lax.all_gather(lax.all_gather(w_d[layer_idx], 'wy', axis=0, tiled=True), 'wx', axis=1, tiled=True)
+            full_gu = lax.all_gather(w_gu[layer_idx], 'wx', axis=0, tiled=True)
+            full_o = lax.all_gather(w_o[layer_idx], 'wx', axis=1, tiled=True)
+            full_d = lax.all_gather(w_d[layer_idx], 'wx', axis=1, tiled=True)
             resid, k_rot, v_val = decoder_layer(resid, gamma_ln[layer_idx], full_q, full_kv, full_gu, full_o, full_d, cos_tab, sin_tab)
             key_list.append(k_rot)
             value_list.append(v_val)

time: 1560 us -> 605 us (0.39)
  waiting for transfers between devices: 1410 us -> 472 us
  matrix products: 107 us -> 80.7 us
    all_gather x16 -> x10, waiting for transfers between devices: 1380 us -> 364 us  [the longest x2 155 us: device_step(): full_gu = lax.all_gather(w_gu[layer_idx], 'wx', axis=0, tiled=True)]
    reduce_scatter x0 -> x2, waiting for transfers between devices: none -> 86 us  [decoder_layer(): mixed = lax.psum_scatter(partial, 'wy', scatter_dimension=0, tiled=True)]
    dot_general x6, matrix products: 61.1 us -> 40.8 us  [the longest x2 28.7 us: decoder_layer(): jnp.einsum('bsd,dcf->bscf', group, w_gu, preferred_element_type=jnp.float32)]
  transfers between devices with their start and end apart: 18 -> 14, of which waited for: 18 -> 14; matrix products, arithmetic and copies ran while one was open for 7% -> 17% of each run, Pallas kernels for 0% -> 0%
where the time goes in v1:
time: 605 us
  waiting for transfers between devices  472 us (78%)
  matrix products  80.7 us (13%)
  local copies, waits for them, and re-layouts  22.8 us (4%)
  between operations  14.2 us (2%)
  other arithmetic  13.3 us (2%)
    all_gather x2, waiting for transfers between devices, device_step(): full_gu = lax.all_gather(w_gu[layer_idx], 'wx', axis=0, tiled=True)  155 us
    reduce_scatter x2, waiting for transfers between devices, decoder_layer(): mixed = lax.psum_scatter(partial, 'wy', scatter_dimension=0, tiled=True)  86 us
    all_gather x2, waiting for transfers between devices, device_step(): full_d = lax.all_gather(w_d[layer_idx], 'wx', axis=1, tiled=True)  76 us
    all_gather x2, waiting for transfers between devices, decoder_layer(): group = lax.all_gather(normed, 'wy', axis=0, tiled=True)  61 us
    all_gather x2, waiting for transfers between devices, device_step(): full_q = lax.all_gather(w_q[layer_idx], 'wx', axis=0, tiled=True)  42.6 us
    all_gather x2, waiting for transfers between devices, device_step(): full_o = lax.all_gather(w_o[layer_idx], 'wx', axis=1, tiled=True)  29.7 us
    dot_general x2, matrix products, decoder_layer(): jnp.einsum('bsd,dcf->bscf', group, w_gu, preferred_element_type=jnp.float32)  28.7 us
    dot_general x2, matrix products, decoder_layer(): jnp.einsum('bsf,fd->bsd', hidden, w_d, preferred_element_type=jnp.float32)  22.9 us
  transfers between devices with their start and end apart: 14, of which 14 were waited for; matrix products, arithmetic and copies ran while one was open for 17% of the time, Pallas kernels for 0%

profile of v1, /device:TPU:97, one launch (start us, length us, event | category | flops | bytes accessed | tf_op | source)
XLA Modules:
  0.0 604.7 jit_solution(15634954719557526714)
XLA Ops:
  7.2 1.2 fusion.179
  8.4 0.8 copy.92
  9.3 1.2 convert_reduce_fusion.1
  10.5 1.3 fusion.69
  11.8 0.8 fusion.180
  12.7 2.2 fusion.71
  15.0 1.9 fusion.175
  17.0 4.7 fusion.171
  21.7 2.3 copy.95
  24.1 3.0 fusion.172
  27.2 0.8 fusion.173
  29.4 5.1 all-gather.27.cloned.1.call-done
  34.5 30.5 %all-gather.23.cloned.1.call-done = bf16[4,128,2048]{2,1,0:T(8,128)(2,1)} async-done(((bf16[1,128,2048]{2,1,0:T(8,128)(2,1)}), bf16[4,128,2048]{2,1,0:T(8,128)(2,1)}) %all-gather.23.cloned.1.call-update) | async-done | bytes 2097168 | tf_op jit(solution)/shard_map/all_gather | solution.py:46
  65.0 2.6 fusion.60
  67.6 0.7 fusion.177
  68.3 0.7 fusion.95
  69.0 20.7 %all-gather.29.cloned.1.call-done = bf16[1,2048,512]{2,1,0:T(8,128)(2,1)} async-done(((bf16[1,256,512]{2,1,0:T(8,128)(2,1)}), bf16[1,2048,512]{2,1,0:T(8,128)(2,1)}) %all-gather.29.cloned.1.call-update) | async-done | bytes 2097168 | tf_op jit(solution)/shard_map/all_gather | solution.py:76
  89.8 3.5 fusion.50
  94.2 0.8 copy-done.1
  95.0 1.5 fusion.181
  96.5 2.0 convolution_convert_fusion.1
  98.5 76.0 %all-gather.33.cloned.1.call-done = bf16[1,2048,2,2048]{3,1,2,0:T(8,128)(2,1)} async-done(((bf16[1,256,2,2048]{3,1,2,0:T(8,128)(2,1)}), bf16[1,2048,2,2048]{3,1,2,0:T(8,128)(2,1)}) %all-gather.33.cloned.1.call-update) | async-done | bytes 16777232 | tf_op jit(solution)/shard_map/all_gather | solution.py:78
  174.5 14.3 %fusion.20 = bf16[4,128,2,2048]{3,1,2,0:T(8,128)(2,1)} fusion(bf16[1,2048,2,2048]{3,1,2,0:T(8,128)(2,1)} %all-gather.33.cloned.1.call-done, bf16[4,128,2048]{2,1,0:T(8,128)(2,1)} %all-gather.23.cloned.1.call-done), kind=kOutput, calls=%fused_computation.24 | convolution fusion | flops 8592031744 | bytes 23068672 | tf_op jit(solution)/shard_map/bsd,dcf->bscf/dot_general | solution.py:50
  188.8 38.0 %all-gather.35.cloned.1.call-done = bf16[1,2048,2048]{2,1,0:T(8,128)(2,1)} async-done(((bf16[1,2048,256]{2,1,0:T(8,128)(2,1)}), bf16[1,2048,2048]{2,1,0:T(8,128)(2,1)}) %all-gather.35.cloned.1.call-update) | async-done | bytes 8388624 | tf_op jit(solution)/shard_map/all_gather | solution.py:80
  226.8 11.4 %fusion.8 = f32[4,128,2048]{2,1,0:T(8,128)} fusion(bf16[1,2048,2048]{2,1,0:T(8,128)(2,1)} %all-gather.35.cloned.1.call-done, bf16[4,128,2,2048]{3,1,2,0:T(8,128)(2,1)} %fusion.20), kind=kOutput, calls=%fused_computation.8 | convolution fusion | flops 4303355904 | bytes 16777216 | tf_op jit(solution)/shard_map/bsf,fd->bsd/dot_general | solution.py:56
  238.3 14.8 %all-gather.31.cloned.1.call-done = bf16[1,512,2048]{2,1,0:T(8,128)(2,1)} async-done(((bf16[1,512,256]{2,1,0:T(8,128)(2,1)}), bf16[1,512,2048]{2,1,0:T(8,128)(2,1)}) %all-gather.31.cloned.1.call-update) | async-done | bytes 2097168 | tf_op jit(solution)/shard_map/all_gather | solution.py:79
  253.0 6.1 %convolution_add_fusion.1 = f32[4,128,2048]{2,1,0:T(8,128)} fusion(f32[4,128,2048]{2,1,0:T(8,128)} %fusion.8, bf16[4,128,512]{1,2,0:T(8,128)(2,1)S(1)} %bitcast.187, bf16[1,512,2048]{2,1,0:T(8,128)(2,1)} %all-gather.31.cloned.1.call-done), kind=kOutput, calls=%fused_computation.27 | convolution fusion | flops 1074790400 | bytes 11010048 | tf_op jit(solution)/shard_map/bsn,nd->bsd/dot_general | solution.py:56
  259.2 0.8 copy.97
  260.1 43.8 %reduce-scatter.3.cloned.1.call-done = f32[1,128,2048]{2,1,0:T(8,128)} async-done(((f32[4,128,2048]{2,1,0:T(8,128)}), f32[1,128,2048]{2,1,0:T(8,128)}) %reduce-scatter.3.cloned.1.call-update) | async-done | bytes 1048592 | tf_op jit(solution)/shard_map/reduce_scatter | solution.py:57
  304.0 1.4 convert_reduce_fusion
  305.7 1.2 fusion.68
  307.6 2.2 copy.100
  310.6 0.7 all-gather.41.cloned.1.call-update
  311.7 14.8 %all-gather.37.cloned.1.call-done = bf16[1,2048,2,128]{1,3,2,0:T(8,128)(2,1)} async-done(((bf16[1,256,2,128]{1,3,2,0:T(8,128)(2,1)}), bf16[1,2048,2,128]{1,3,2,0:T(8,128)(2,1)}) %all-gather.37.cloned.1.call-update) | async-done | bytes 1048592 | tf_op jit(solution)/shard_map/all_gather | solution.py:77
  326.5 30.5 %all-gather.25.cloned.1.call-done = bf16[4,128,2048]{2,1,0:T(8,128)(2,1)} async-done(((bf16[1,128,2048]{2,1,0:T(8,128)(2,1)}), bf16[4,128,2048]{2,1,0:T(8,128)(2,1)}) %all-gather.25.cloned.1.call-update) | async-done | bytes 2097168 | tf_op jit(solution)/shard_map/all_gather | solution.py:46
  357.0 2.6 fusion.63
  359.7 21.9 %all-gather.39.cloned.1.call-done = bf16[1,2048,512]{2,1,0:T(8,128)(2,1)} async-done(((bf16[1,256,512]{2,1,0:T(8,128)(2,1)}), bf16[1,2048,512]{2,1,0:T(8,128)(2,1)}) %all-gather.39.cloned.1.call-update) | async-done | bytes 2097168 | tf_op jit(solution)/shard_map/all_gather | solution.py:76
  381.6 3.5 fusion.53
  387.0 0.8 convolution_convert_fusion
  387.8 78.6 %all-gather.43.cloned.1.call-done = bf16[1,2048,2,2048]{3,1,2,0:T(8,128)(2,1)} async-done(((bf16[1,256,2,2048]{3,1,2,0:T(8,128)(2,1)}), bf16[1,2048,2,2048]{3,1,2,0:T(8,128)(2,1)}) %all-gather.43.cloned.1.call-update) | async-done | bytes 16777232 | tf_op jit(solution)/shard_map/all_gather | solution.py:78
  466.4 14.3 %fusion.23 = bf16[4,128,2,2048]{3,1,0,2:T(8,128)(2,1)} fusion(bf16[1,2048,2,2048]{3,1,2,0:T(8,128)(2,1)} %all-gather.43.cloned.1.call-done, bf16[4,128,2048]{2,1,0:T(8,128)(2,1)} %all-gather.25.cloned.1.call-done), kind=kOutput, calls=%fused_computation.25 | convolution fusion | flops 8592031744 | bytes 23068672 | tf_op jit(solution)/shard_map/bsd,dcf->bscf/dot_general | solution.py:50
  480.8 38.0 %all-gather.45.cloned.1.call-done = bf16[1,2048,2048]{2,1,0:T(8,128)(2,1)} async-done(((bf16[1,2048,256]{2,1,0:T(8,128)(2,1)}), bf16[1,2048,2048]{2,1,0:T(8,128)(2,1)}) %all-gather.45.cloned.1.call-update) | async-done | bytes 8388624 | tf_op jit(solution)/shard_map/all_gather | solution.py:80
  518.8 11.4 %fusion.6 = f32[4,128,2048]{2,1,0:T(8,128)} fusion(bf16[1,2048,2048]{2,1,0:T(8,128)(2,1)} %all-gather.45.cloned.1.call-done, bf16[4,128,2,2048]{3,1,0,2:T(8,128)(2,1)} %fusion.23), kind=kOutput, calls=%fused_computation.6 | convolution fusion | flops 4303355904 | bytes 16777216 | tf_op jit(solution)/shard_map/bsf,fd->bsd/dot_general | solution.py:56
  530.2 14.9 %all-gather.41.cloned.1.call-done = bf16[1,512,2048]{2,1,0:T(8,128)(2,1)} async-done(((bf16[1,512,256]{2,1,0:T(8,128)(2,1)}), bf16[1,512,2048]{2,1,0:T(8,128)(2,1)}) %all-gather.41.cloned.1.call-update) | async-done | bytes 2097168 | tf_op jit(solution)/shard_map/all_gather | solution.py:79
  545.2 6.1 %convolution_add_fusion = f32[4,128,2048]{2,1,0:T(8,128)} fusion(f32[4,128,2048]{2,1,0:T(8,128)} %fusion.6, bf16[4,128,512]{1,2,0:T(8,128)(2,1)S(1)} %bitcast.186, bf16[1,512,2048]{2,1,0:T(8,128)(2,1)} %all-gather.41.cloned.1.call-done), kind=kOutput, calls=%fused_computation.26 | convolution fusion | flops 1074790400 | bytes 11010048 | tf_op jit(solution)/shard_map/bsn,nd->bsd/dot_general | solution.py:56
  551.3 0.8 constant_dynamic-slice_fusion.1
  553.9 42.2 %reduce-scatter.5.cloned.1.call-done = f32[1,128,2048]{2,1,0:T(8,128)} async-done(((f32[4,128,2048]{2,1,0:T(8,128)}), f32[1,128,2048]{2,1,0:T(8,128)}) %reduce-scatter.5.cloned.1.call-update) | async-done | bytes 1048592 | tf_op jit(solution)/shard_map/reduce_scatter | solution.py:57
  596.1 2.1 fusion.81
  (67 shorter events, 9.1 us)
Async XLA Ops:
  7.2 27.3 %all-gather.27.cloned.1.call-start = ((), (), s32[]{:S(2)}) async-start(), calls=%async_computation.6 | async-start | bytes 1179648 | tf_op jit(solution)/shard_map/all_gather | solution.py:77
  9.2 55.8 %all-gather.23.cloned.1.call-start = ((), (), s32[]{:S(2)}) async-start(), calls=%async_computation.2 | async-start | bytes 2621440 | tf_op jit(solution)/shard_map/all_gather | solution.py:46
  14.9 74.8 %all-gather.29.cloned.1.call-start = ((), (), s32[]{:S(2)}) async-start(), calls=%async_computation.7 | async-start | bytes 2359296 | tf_op jit(solution)/shard_map/all_gather | solution.py:76
  16.9 157.5 %all-gather.33.cloned.1.call-start = ((), (), s32[]{:S(2)}) async-start(), calls=%async_computation.9 | async-start | bytes 18874368 | tf_op jit(solution)/shard_map/all_gather | solution.py:78
  23.9 3.3 copy-start.2
  24.0 202.8 %all-gather.35.cloned.1.call-start = ((), (), s32[]{:S(2)}) async-start(), calls=%async_computation.10 | async-start | bytes 9437184 | tf_op jit(solution)/shard_map/all_gather | solution.py:80
  27.2 225.9 %all-gather.31.cloned.1.call-start = ((), (), s32[]{:S(2)}) async-start(), calls=%async_computation.8 | async-start | bytes 2359296 | tf_op jit(solution)/shard_map/all_gather | solution.py:79
  28.1 275.8 %reduce-scatter.3.cloned.1.call-start = ((), (), s32[]{:S(2)}) async-start(), calls=%async_computation.3 | async-start | bytes 5242880 | tf_op jit(solution)/shard_map/reduce_scatter | solution.py:57
  67.6 1.4 copy-start.4
  94.2 0.8 copy-start.1
  259.1 44.8 %copy-start = (bf16[1,128,2048]{2,1,0:T(8,128)(2,1)S(1)}, bf16[1,128,2048]{2,1,0:T(8,128)(2,1)}, u32[]{:S(2)}) copy-start(bf16[1,128,2048]{2,1,0:T(8,128)(2,1)} %param.7) | copy-start | bytes 1572868
  259.2 67.3 %all-gather.37.cloned.1.call-start = ((), (), s32[]{:S(2)}) async-start(), calls=%async_computation.11 | async-start | bytes 1179648 | tf_op jit(solution)/shard_map/all_gather | solution.py:77
  260.1 96.9 %all-gather.25.cloned.1.call-start = ((), (), s32[]{:S(2)}) async-start(), calls=%async_computation.4 | async-start | bytes 2621440 | tf_op jit(solution)/shard_map/all_gather | solution.py:46
  306.9 74.6 %all-gather.39.cloned.1.call-start = ((), (), s32[]{:S(2)}) async-start(), calls=%async_computation.12 | async-start | bytes 2359296 | tf_op jit(solution)/shard_map/all_gather | solution.py:76
  307.6 158.9 %all-gather.43.cloned.1.call-start = ((), (), s32[]{:S(2)}) async-start(), calls=%async_computation.14 | async-start | bytes 18874368 | tf_op jit(solution)/shard_map/all_gather | solution.py:78
  309.9 208.9 %all-gather.45.cloned.1.call-start = ((), (), s32[]{:S(2)}) async-start(), calls=%async_computation.15 | async-start | bytes 9437184 | tf_op jit(solution)/shard_map/all_gather | solution.py:80
  310.6 234.6 %all-gather.41.cloned.1.call-start = ((), (), s32[]{:S(2)}) async-start(), calls=%async_computation.13 | async-start | bytes 2359296 | tf_op jit(solution)/shard_map/all_gather | solution.py:79
  311.4 284.7 %reduce-scatter.5.cloned.1.call-start = ((), (), s32[]{:S(2)}) async-start(), calls=%async_computation.5 | async-start | bytes 5242880 | tf_op jit(solution)/shard_map/reduce_scatter | solution.py:57
  385.0 1.3 copy-start.5
  551.2 1.0 copy-start.3
Sparse Core Ops, SparseCore 0:
  9.6 24.8 all-gather.26
  36.6 28.3 all-gather.22
  66.6 23.0 all-gather.28
  91.2 83.2 all-gather.32
  175.9 50.8 all-gather.34
  228.3 24.7 all-gather.30
  259.3 44.6 reduce-scatter.2
  305.5 20.8 all-gather.36
  328.6 28.3 all-gather.24
  358.4 23.0 all-gather.38
  383.2 83.2 all-gather.42
  467.9 50.8 all-gather.44
  520.4 24.7 all-gather.40
  551.4 44.6 reduce-scatter.4

commit v2 on v0

v2 whole, which is shorter than its diff:
```python
import functools

import jax
import jax.numpy as jnp
from jax import lax
from jax.experimental import pallas as pl
from jax.experimental.pallas import tpu as pltpu
from jax.sharding import PartitionSpec as P

LN_EPS = 1e-6
ROPE_BASE = 10000.0
CORES = 2
GU_CHUNKS = 4
HALVES = 2
BF, F32 = jnp.bfloat16, jnp.float32

LOCAL, SIB, L0, L1, R0, R1, FL, FR = range(8)
A_SIB, A_L, A_R, A_TOP, A_BOT, A_SL, A_SR, A_STOP, A_SBOT = range(9)


def rope_tables(seq_len, head_dim):
    half_dim = head_dim // 2
    inv_freq = ROPE_BASE ** (-2.0 * jnp.arange(half_dim, dtype=F32) / head_dim)
    angles = jnp.arange(seq_len, dtype=F32)[:, None] * inv_freq[None, :]
    return jnp.cos(angles), jnp.sin(angles)


def layers_kernel(dims, x_ref, gamma_ref, cos_ref, sin_ref, wqkv, wgu, wo, wd,
                  y_out, k_out, v_out,
                  bqkv, bgu, bo, bd, hbuf, qbuf, kvbuf, obuf, mbuf, part, rs0, rs1, rs2, resid,
                  w_send, w_recv, a_send, a_recv, kv_send, kv_recv, r_send, r_recv, out_sem):
    layers, n_x, n_y, seq, head_dim, rows, width = dims
    heads = wo.shape[1] // CORES // head_dim
    hid = wd.shape[1] // CORES
    o_rows = wo.shape[1] // CORES
    q_cols = heads * head_dim
    g_cols = wgu.shape[-1] // 2
    n_prompts = CORES * n_y
    toks = n_prompts * seq
    keep = n_y * seq
    tile = toks // 4

    wx = lax.axis_index('wx')
    y = lax.axis_index('wy')
    x, c = wx // CORES, wx % CORES
    xr, xl, xo = (x + 1) % n_x, (x + n_x - 1) % n_x, (x + 2) % n_x
    yr, yl, yo = (y + 1) % n_y, (y + n_y - 1) % n_y, (y + 2) % n_y
    sibling = {'wx': x * CORES + 1 - c}
    right_y, left_y = {'wy': yr}, {'wy': yl}

    def at_x(chip, core):
        return {'wx': chip * CORES + core}

    barrier = pltpu.get_barrier_semaphore()
    peers = [sibling, right_y, left_y] + [at_x(chip, core) for chip in (xr, xl) for core in range(CORES)]
    for peer in peers:
        pl.semaphore_signal(barrier, inc=1, device_id=peer, device_id_type=pl.DeviceIdType.MESH)
    pl.semaphore_wait(barrier, len(peers))

    def remote(src, dst, send_sem, recv_sem, peer):
        return pltpu.make_async_remote_copy(src_ref=src, dst_ref=dst, send_sem=send_sem, recv_sem=recv_sem,
                                            device_id=peer, device_id_type=pl.DeviceIdType.MESH)

    def wait_in(ref, recv_sem, send_sem):
        remote(ref, ref, send_sem, recv_sem, sibling).wait_recv()

    def wait_out(ref, recv_sem, send_sem):
        remote(ref, ref, send_sem, recv_sem, sibling).wait_send()

    pieces = []
    n_blocks = 0
    for l in range(layers):
        pieces.append([('qkv', l, 0, n_blocks)])
        n_blocks += 1
        for j in range(GU_CHUNKS):
            pieces.append([('gu', l, j, n_blocks)])
            n_blocks += 1
        for hh in range(HALVES):
            pieces.append([('o', l, hh, n_blocks), ('d', l, hh, n_blocks + 1)])
            n_blocks += 2
    per_layer = len(pieces) // layers

    def source(block, core):
        kind, l, j, _ = block
        if kind == 'qkv':
            return wqkv.at[l, core]
        if kind == 'gu':
            return wgu.at[l, core, j]
        if kind == 'o':
            return wo.at[l, pl.ds(pl.multiple_of(core * o_rows, o_rows), o_rows), pl.ds(j * width, width)]
        return wd.at[l, pl.ds(pl.multiple_of(core * hid, hid), hid), pl.ds(j * width, width)]

    def landing(block, chip, core):
        kind, l, j, _ = block
        row = pl.ds(pl.multiple_of((chip * CORES + core) * rows, rows), rows)
        col = pl.ds(pl.multiple_of(core * width, width), width)
        if kind == 'qkv':
            return bqkv.at[l, row]
        if kind == 'gu':
            return bgu.at[l, j, row]
        if kind == 'o':
            return bo.at[l, j, chip, :, col]
        return bd.at[l, j, chip, :, col]

    def issue_own(p):
        if p >= len(pieces):
            return
        for block in pieces[p]:
            t = block[3]
            here = landing(block, x, c)
            for core in range(CORES):
                remote(source(block, core), here, w_send.at[t, 2 + core], w_recv.at[t, L0 + c], at_x(xr, core)).start()
                remote(source(block, core), here, w_send.at[t, 4 + core], w_recv.at[t, R0 + c], at_x(xl, core)).start()
            remote(source(block, 1 - c), here, w_send.at[t, SIB], w_recv.at[t, SIB], sibling).start()
            pltpu.make_async_copy(source(block, c), here, w_recv.at[t, LOCAL]).start()

    def wait_block(block, how):
        t = block[3]
        if how == LOCAL:
            pltpu.make_async_copy(source(block, c), landing(block, x, c), w_recv.at[t, LOCAL]).wait()
            return
        chip, core = {SIB: (x, 1 - c), L0: (xl, 0), L1: (xl, 1), R0: (xr, 0), R1: (xr, 1), FL: (xo, 0), FR: (xo, 1)}[how]
        wait_in(landing(block, chip, core), w_recv.at[t, how], w_send.at[t, 0])

    done = [0]

    def comm(p):
        if p >= len(pieces):
            return
        assert p == done[0]
        done[0] = p + 1
        for block in pieces[p]:
            t = block[3]
            wait_block(block, L0)
            from_left = landing(block, xl, 0)
            remote(from_left, from_left, w_send.at[t, 6], w_recv.at[t, FL], at_x(xr, c)).start()
            wait_block(block, R1)
            from_right = landing(block, xr, 1)
            remote(from_right, from_right, w_send.at[t, 7], w_recv.at[t, FR], at_x(xl, c)).start()
        issue_own(p + 2)

    def wait_piece(p, hows):
        for block in pieces[p]:
            for how in hows:
                wait_block(block, how)

    def drain_weights():
        for piece in pieces:
            for block in piece:
                for kind in range(1, 8):
                    wait_out(landing(block, x, c), w_recv.at[block[3], SIB], w_send.at[block[3], kind])

    def prompt(slot, part_of=None):
        if part_of is None:
            return hbuf.at[pl.ds(pl.multiple_of(slot * seq, seq), seq)]
        half = seq // 2
        return hbuf.at[pl.ds(pl.multiple_of(slot * seq + part_of * half, half), half)]

    def a_copy(l, src, dst, kind, peer):
        remote(src, dst, a_send.at[l, kind], a_recv.at[l, kind], peer).start()

    def a_wait(l, ref, kind):
        wait_in(ref, a_recv.at[l, kind], a_send.at[l, kind])

    def gather_send(l):
        a_copy(l, prompt(y), prompt(y), A_L, right_y)
        a_copy(l, prompt(y), prompt(y), A_R, left_y)
        a_copy(l, prompt(y), prompt(n_y + y), A_SIB, sibling)

    def gather_forward(l):
        a_wait(l, prompt(yl), A_L)
        a_copy(l, prompt(yl, 0), prompt(yl, 0), A_TOP, right_y)
        a_copy(l, prompt(yl), prompt(n_y + yl), A_SL, sibling)
        a_wait(l, prompt(yr), A_R)
        a_copy(l, prompt(yr, 1), prompt(yr, 1), A_BOT, left_y)
        a_copy(l, prompt(yr), prompt(n_y + yr), A_SR, sibling)

    def gather_share(l):
        a_wait(l, prompt(yo, 0), A_TOP)
        a_copy(l, prompt(yo, 0), prompt(n_y + yo, 0), A_STOP, sibling)
        a_wait(l, prompt(yo, 1), A_BOT)
        a_copy(l, prompt(yo, 1), prompt(n_y + yo, 1), A_SBOT, sibling)

    def gather_finish(l):
        a_wait(l, prompt(n_y + y), A_SIB)
        a_wait(l, prompt(n_y + yl), A_SL)
        a_wait(l, prompt(n_y + yr), A_SR)
        a_wait(l, prompt(n_y + yo, 0), A_STOP)
        a_wait(l, prompt(n_y + yo, 1), A_SBOT)

    def gather_drain(l):
        for kind in (A_L, A_R, A_SIB, A_SL, A_SR):
            wait_out(prompt(y), a_recv.at[l, kind], a_send.at[l, kind])
        for kind in (A_TOP, A_BOT, A_STOP, A_SBOT):
            wait_out(prompt(y, 0), a_recv.at[l, kind], a_send.at[l, kind])

    n_res = resid.shape[0]
    d_model = n_res * width

    def norm_own(l):
        total = jnp.zeros((seq, 1), F32)
        for i in range(n_res):
            total += jnp.sum(resid[i].astype(F32), axis=-1, keepdims=True)
        mean = total / d_model
        square = jnp.zeros((seq, 1), F32)
        for i in range(n_res):
            centered = resid[i].astype(F32) - mean
            square += jnp.sum(centered * centered, axis=-1, keepdims=True)
        scale = lax.rsqrt(square / d_model + LN_EPS)
        own = pl.ds(pl.multiple_of(y * seq, seq), seq)
        for i in range(n_res):
            value = (resid[i].astype(F32) - mean) * scale * gamma_ref[l, i]
            hbuf[own, i * width:(i + 1) * width] = value.astype(BF)

    def rotate(value):
        value = value.astype(F32)
        return (value * cos_ref[...] + pltpu.roll(value, head_dim // 2, 1) * sin_ref[...]).astype(BF)

    def tiles(body, n=4, size=tile):
        def step(i, carry):
            body(pl.multiple_of(i * size, size))
            return carry
        lax.fori_loop(0, n, step, 0)

    def project_qkv(l):
        def body(start):
            at = pl.ds(start, tile)
            acc = jnp.dot(hbuf[at, :], bqkv[l], preferred_element_type=F32).astype(BF)
            for n in range(heads):
                qbuf[at, n * head_dim:(n + 1) * head_dim] = rotate(acc[:, n * head_dim:(n + 1) * head_dim])
            kv = acc[:, q_cols:]
            kvbuf[c, at, :] = jnp.where(c == 0, rotate(kv), kv)
        tiles(body)

    def kv_refs(lo):
        return kvbuf.at[c, pl.ds(lo * keep, keep)]

    def kv_exchange(l):
        for lo in range(2):
            remote(kv_refs(lo), kv_refs(1 - lo), kv_send.at[l, lo], kv_recv.at[l, lo], sibling).start()

    def kv_outs(l):
        own = pl.ds(pl.multiple_of(y * seq, seq), seq)
        return [pltpu.make_async_copy(kvbuf.at[0, own], k_out.at[l, 0], out_sem.at[2 * l]),
                pltpu.make_async_copy(kvbuf.at[1, own], v_out.at[l, 0], out_sem.at[2 * l + 1])]

    def kv_finish(l):
        for lo in range(2):
            wait_in(kvbuf.at[1 - c, pl.ds((1 - lo) * keep, keep)], kv_recv.at[l, lo], kv_send.at[l, lo])
        for copy in kv_outs(l):
            copy.start()

    def kv_drain(l):
        for lo in range(2):
            wait_out(kv_refs(lo), kv_recv.at[l, lo], kv_send.at[l, lo])
        for copy in kv_outs(l):
            copy.wait()

    def attend():
        score_scale = head_dim ** -0.5
        allowed = lax.broadcasted_iota(jnp.int32, (seq, seq), 0) >= lax.broadcasted_iota(jnp.int32, (seq, seq), 1)

        def body(start):
            at = pl.ds(start, seq)
            key, val = kvbuf[0, at, :], kvbuf[1, at, :]
            for n in range(heads):
                query = qbuf[at, n * head_dim:(n + 1) * head_dim]
                scores = lax.dot_general(query, key, (((1,), (1,)), ((), ())), preferred_element_type=F32) * score_scale
                scores = jnp.where(allowed, scores, -jnp.inf)
                weights = jnp.exp(scores - jnp.max(scores, axis=-1, keepdims=True))
                probs = (weights / jnp.sum(weights, axis=-1, keepdims=True)).astype(BF)
                obuf[at, n * head_dim:(n + 1) * head_dim] = jnp.dot(probs, val, preferred_element_type=F32).astype(BF)
        tiles(body, n_prompts, seq)

    def gate_up(l, j):
        def body(start):
            at = pl.ds(start, tile)
            acc = jnp.dot(hbuf[at, :], bgu[l, j], preferred_element_type=F32).astype(BF).astype(F32)
            mbuf[at, j * g_cols:(j + 1) * g_cols] = (jax.nn.silu(acc[:, :g_cols]) * acc[:, g_cols:]).astype(BF)
        tiles(body)

    chips = [x, xl, xr, xo]
    half_w = width

    def chunk(b, hh):
        return b * HALVES + hh

    def project_out(l, b, hh):
        k = chunk(b, hh)

        def body(start):
            at = pl.ds(start, tile)
            part[k, at, :] = (jnp.dot(obuf[at, :], bo[l, hh, chips[b]], preferred_element_type=F32)
                              + jnp.dot(mbuf[at, :], bd[l, hh, chips[b]], preferred_element_type=F32))

        def step(i, carry):
            body(pl.multiple_of(((i + 2) % 4) * tile, tile))
            return carry
        lax.fori_loop(0, 4, step, 0)
        remote(part.at[k, pl.ds(keep, keep)], rs0.at[k], r_send.at[k, 0], r_recv.at[k, 0], sibling).start()

    def of_chip(k, yy):
        return part.at[k, pl.ds(pl.multiple_of(yy * seq, seq), seq)]

    def of_chip_half(k, yy, side):
        return part.at[k, pl.ds(pl.multiple_of(yy * seq, seq), seq), pl.ds(side * half_w, half_w)]

    def reduce_cores(b, hh):
        k = chunk(b, hh)
        wait_in(rs0.at[k], r_recv.at[k, 0], r_send.at[k, 0])
        part[k, 0:keep, :] += rs0[k]
        remote(of_chip_half(k, yo, 0), rs1.at[k, 0], r_send.at[k, 1], r_recv.at[k, 1], right_y).start()
        remote(of_chip_half(k, yo, 1), rs1.at[k, 1], r_send.at[k, 2], r_recv.at[k, 2], left_y).start()

    def reduce_far(b, hh):
        k = chunk(b, hh)
        for side, target, peer in ((0, yr, right_y), (1, yl, left_y)):
            wait_in(rs1.at[k, side], r_recv.at[k, 1 + side], r_send.at[k, 1 + side])
            at = pl.ds(pl.multiple_of(target * seq, seq), seq)
            part[k, at, side * half_w:(side + 1) * half_w] += rs1[k, side]
            remote(of_chip(k, target), rs2.at[k, side], r_send.at[k, 3 + side], r_recv.at[k, 3 + side], peer).start()

    def out_copy(i, k, core):
        return pltpu.make_async_copy(resid.at[i], y_out.at[0, :, pl.ds(pl.multiple_of(i * width, width), width)],
                                     out_sem.at[2 * layers + CORES * k + core])

    def reduce_last(l, b, hh):
        k = chunk(b, hh)
        for side in range(2):
            wait_in(rs2.at[k, side], r_recv.at[k, 3 + side], r_send.at[k, 3 + side])
        own = pl.ds(pl.multiple_of(y * seq, seq), seq)
        total = part[k, own, :] + rs2[k, 0] + rs2[k, 1]
        for core in range(CORES):
            i = (chips[b] * CORES + core) * HALVES + hh
            resid[i] = (resid[i].astype(F32) + total[:, core * width:(core + 1) * width]).astype(BF)
            if l == layers - 1:
                out_copy(i, k, core).start()

    def reduce_drain():
        for k in range(len(chips) * HALVES):
            wait_out(rs0.at[k], r_recv.at[k, 0], r_send.at[k, 0])
            for side in range(2):
                wait_out(rs1.at[k, side], r_recv.at[k, 1 + side], r_send.at[k, 1 + side])
                wait_out(rs2.at[k, side], r_recv.at[k, 3 + side], r_send.at[k, 3 + side])

    issue_own(0)
    issue_own(1)
    for i in range(n_res):
        resid[i] = x_ref[0, :, i * width:(i + 1) * width]
    norm_own(0)
    gather_send(0)
    comm(0)
    gather_forward(0)
    gather_share(0)
    gather_finish(0)
    rest = (LOCAL, SIB, L1, R0, FL, FR)
    OWN, LEFT, RIGHT, FAR = range(4)
    for l in range(layers):
        base = l * per_layer
        last = l == layers - 1

        def ahead(p):
            while done[0] <= p:
                comm(done[0])

        ahead(base + 1)
        wait_piece(base, rest)
        project_qkv(l)
        kv_exchange(l)
        ahead(base + 2)
        wait_piece(base + 1, rest)
        gate_up(l, 0)
        kv_finish(l)
        attend()
        for j in range(1, GU_CHUNKS):
            ahead(base + 2 + j)
            wait_piece(base + 1 + j, rest)
            gate_up(l, j)
        gather_drain(l)
        kv_drain(l)
        c0, c1 = base + 1 + GU_CHUNKS, base + 2 + GU_CHUNKS
        wait_piece(c0, (LOCAL, SIB))
        project_out(l, OWN, 0)
        wait_piece(c1, (LOCAL, SIB))
        project_out(l, OWN, 1)
        reduce_cores(OWN, 0)
        wait_piece(c0, (L1, R0))
        project_out(l, LEFT, 0)
        reduce_cores(OWN, 1)
        reduce_far(OWN, 0)
        project_out(l, RIGHT, 0)
        reduce_cores(LEFT, 0)
        reduce_far(OWN, 1)
        reduce_cores(RIGHT, 0)
        reduce_last(l, OWN, 0)
        reduce_far(LEFT, 0)
        comm(c1)
        wait_piece(c1, (L1, R0))
        project_out(l, LEFT, 1)
        reduce_far(RIGHT, 0)
        reduce_last(l, OWN, 1)
        project_out(l, RIGHT, 1)
        reduce_cores(LEFT, 1)
        wait_piece(c0, (FL, FR))
        project_out(l, FAR, 0)
        reduce_cores(RIGHT, 1)
        reduce_last(l, LEFT, 0)
        reduce_far(LEFT, 1)
        if not last:
            comm(c1 + 1)
        wait_piece(c1, (FL, FR))
        project_out(l, FAR, 1)
        reduce_cores(FAR, 0)
        reduce_last(l, RIGHT, 0)
        reduce_far(RIGHT, 1)
        reduce_cores(FAR, 1)
        reduce_last(l, LEFT, 1)
        reduce_far(FAR, 0)
        reduce_last(l, RIGHT, 1)
        reduce_far(FAR, 1)
        reduce_last(l, FAR, 0)
        reduce_last(l, FAR, 1)
        reduce_drain()
        if not last:
            norm_own(l + 1)
            comm(c1 + 2)
            gather_send(l + 1)
            gather_forward(l + 1)
            gather_share(l + 1)
            gather_finish(l + 1)
    drain_weights()
    for b in range(len(chips)):
        for hh in range(HALVES):
            for core in range(CORES):
                out_copy((chips[b] * CORES + core) * HALVES + hh, chunk(b, hh), core).wait()


def run_layers(mesh_sizes, x_tokens, gamma_ln, w_q, w_kv, w_gu, w_o, w_d):
    n_x, n_y = mesh_sizes['wx'] // CORES, mesh_sizes['wy']
    assert n_x == 4 and n_y == 4 and x_tokens.shape[0] == 1
    layers, rows, q_loc = w_q.shape
    seq, d_model = x_tokens.shape[1:]
    head_dim = w_kv.shape[-1]
    hid_loc = w_gu.shape[-1]
    hid = hid_loc // CORES
    g_cols = hid // GU_CHUNKS
    q_cols = q_loc // CORES
    width = rows // HALVES
    toks = CORES * n_y * seq
    n_chunks = n_x * HALVES
    n_res = d_model // width
    q_split = jnp.swapaxes(w_q.reshape(layers, rows, CORES, q_cols), 1, 2)
    wqkv = jnp.concatenate([q_split, jnp.swapaxes(w_kv, 1, 2)], axis=-1)
    wgu = w_gu.reshape(layers, rows, 2, CORES, GU_CHUNKS, g_cols).transpose(0, 3, 4, 1, 2, 5)
    wgu = wgu.reshape(layers, CORES, GU_CHUNKS, rows, 2 * g_cols)
    cos_tab, sin_tab = rope_tables(seq, head_dim)
    reps = toks // 4 // seq
    cos_all = jnp.tile(jnp.concatenate([cos_tab, cos_tab], axis=-1), (reps, 1))
    sin_all = jnp.tile(jnp.concatenate([-sin_tab, sin_tab], axis=-1), (reps, 1))
    gamma = gamma_ln.reshape(layers, n_res, 1, width)
    blocks = layers * (1 + GU_CHUNKS + 2 * HALVES)
    dma = pltpu.SemaphoreType.DMA
    in_vmem, anywhere = pl.BlockSpec(memory_space=pltpu.VMEM), pl.BlockSpec(memory_space=pl.ANY)
    cache = jax.ShapeDtypeStruct((layers, 1, seq, head_dim), BF)
    return pl.pallas_call(
        functools.partial(layers_kernel, (layers, n_x, n_y, seq, head_dim, rows, width)),
        out_shape=(jax.ShapeDtypeStruct(x_tokens.shape, BF), cache, cache),
        in_specs=[in_vmem] * 4 + [anywhere] * 4,
        out_specs=(anywhere,) * 3,
        scratch_shapes=[
            pltpu.VMEM((layers, d_model, q_cols + head_dim), BF),
            pltpu.VMEM((layers, GU_CHUNKS, d_model, 2 * g_cols), BF),
            pltpu.VMEM((layers, HALVES, n_x, q_cols, CORES * width), BF),
            pltpu.VMEM((layers, HALVES, n_x, hid, CORES * width), BF),
            pltpu.VMEM((toks, d_model), BF),
            pltpu.VMEM((toks, q_cols), BF),
            pltpu.VMEM((2, toks, head_dim), BF),
            pltpu.VMEM((toks, q_cols), BF),
            pltpu.VMEM((toks, hid), BF),
            pltpu.VMEM((n_chunks, toks, CORES * width), F32),
            pltpu.VMEM((n_chunks, toks // CORES, CORES * width), F32),
            pltpu.VMEM((n_chunks, 2, seq, width), F32),
            pltpu.VMEM((n_chunks, 2, seq, CORES * width), F32),
            pltpu.VMEM((n_res, seq, width), BF),
            dma((blocks, 8)), dma((blocks, 8)),
            dma((layers, 9)), dma((layers, 9)),
            dma((layers, 2)), dma((layers, 2)),
            dma((n_chunks, 5)), dma((n_chunks, 5)),
            dma((2 * layers + CORES * n_chunks,)),
        ],
        compiler_params=pltpu.CompilerParams(collective_id=0, has_side_effects=True, vmem_limit_bytes=67043328),
    )(x_tokens, gamma, cos_all, sin_all, wqkv, wgu, w_o, w_d)


def solution(mesh):
    batch_axes = ('dp', 'wy', 'wx')
    in_specs = (P(batch_axes), P(), P(None, 'wx', 'wy'), P(None, 'wx'), P(None, 'wx', None, 'wy'), P(None, 'wy', 'wx'), P(None, 'wy', 'wx'))
    out_specs = (P(batch_axes), P(None, batch_axes), P(None, batch_axes))
    sizes = dict(mesh.shape)
    return jax.shard_map(functools.partial(run_layers, sizes), mesh=mesh, in_specs=in_specs, out_specs=out_specs, check_vma=False)
```

time: 1560 us -> 306 us (0.20)
  waiting for transfers between devices: 1410 us -> 0 us
  Pallas kernels: 0 us -> 273 us
  matrix products: 107 us -> 0 us
    all_gather x18 -> x0, waiting for transfers between devices: 1410 us -> none  [the longest x2 585 us: device_step(): lax.all_gather(lax.all_gather(w_gu[layer_idx], 'wy', axis=2, tiled=True),...]
    pallas_call x0 -> x1, Pallas kernels: none -> 273 us  [run_layers(): pl.pallas_call(functools.partial(layers_kernel, (layers, n_x, n_y, seq, h...]
    dot_general x12 -> x0, matrix products: 103 us -> none  [the longest x2 50.8 us: decoder_layer(): jnp.einsum('bsd,dcf->bscf', normed, w_gu, preferred_element_type=jnp.floa...]
    reshape x0 -> x5, local copies, waits for them, and re-layouts: none -> 23.8 us  [the longest x2 15.3 us: run_layers(): w_gu.reshape(layers, rows, 2, CORES, GU_CHUNKS, g_cols)]
  transfers between devices with their start and end apart: 18 -> 0, of which waited for: 18 -> 0; matrix products, arithmetic and copies ran while one was open for 7% -> 0% of each run, Pallas kernels for 0% -> 0%
where the time goes in v2:
time: 306 us; the launch traced here: 305 us
  Pallas kernels  273 us (89%)
  local copies, waits for them, and re-layouts  30.2 us (10%)
    pallas_call x1, Pallas kernels, run_layers(): pl.pallas_call(functools.partial(layers_kernel, (layers, n_x, n_y, seq, h...  273 us
    reshape x2, local copies, waits for them, and re-layouts, run_layers(): w_gu.reshape(layers, rows, 2, CORES, GU_CHUNKS, g_cols)  15.3 us
    reshape x1, local copies, waits for them, and re-layouts, run_layers(): wgu = wgu.reshape(layers, CORES, GU_CHUNKS, rows, 2 * g_cols)  7.65 us

profile of v2, /device:TPU:97, one launch (start us, length us, event | category | flops | bytes accessed | tf_op | source)
XLA Modules:
  0.0 305.2 jit_solution(10850039620446598518)
XLA Ops:
  0.6 0.3 fusion.2
  0.9 0.1 pad_maximum_fusion.1
  1.0 0.7 tile.8
  1.7 0.6 tile.20
  2.3 7.6 %reshape.33 = bf16[2,256,2,2,4,256]{5,4,3,2,1,0:T(4,128)(2,1)} reshape(bf16[2,256,2,2048]{3,2,1,0:T(2,128)(2,1)} %param.11) | data formatting | bytes 8388608 | tf_op jit(solution)/shard_map/reshape | solution.py:454
  9.9 7.7 %copy.18 = bf16[2,256,2,2,4,256]{5,2,1,4,3,0:T(2,128)(2,1)} copy(bf16[2,256,2,2,4,256]{5,4,3,2,1,0:T(4,128)(2,1)} %reshape.33) | data formatting | bytes 8388608 | tf_op jit(solution)/shard_map/reshape | solution.py:454
  17.6 0.0 copy-start
  17.6 0.0 copy-start.1
  17.6 7.7 %reshape.34.wgu = bf16[2,2,4,256,512]{4,3,2,1,0:T(8,128)(2,1)} reshape(bf16[2,2,4,256,2,256]{5,4,3,2,1,0:T(2,128)(2,1)} %bitcast.10) | data formatting | bytes 8388608 | tf_op jit(solution)/shard_map/reshape | solution.py:455
  25.3 0.0 copy-done
  25.3 0.0 copy-start.2
  25.3 0.2 copy.12
  25.5 0.2 copy.13
  25.7 0.0 copy-done.1
  25.7 1.0 pad_maximum_fusion.wqkv
  26.7 0.0 copy-done.2
  26.7 0.6 reshape.31.gamma_ref
  27.4 273.0 %shard_map.94 = (bf16[1,128,2048]{2,1,0:T(8,128)(2,1)}, bf16[2,1,128,128]{3,2,1,0:T(8,128)(2,1)}, bf16[2,1,128,128]{3,2,1,0:T(8,128)(2,1)}) custom-call(bf16[1,128,2048]{2,1,0:T(8,128)(2,1)} %x_ref.1, f32[2,16,1,128]{3,2,1,0:T(1,128)} %reshape.31.gamma_ref, f32[256,128]{1,0:T(8,128)} %bitcast.14, f32[256,128]{1,0:T(8,128)} %bitcast.15, ...), custom_call_target="tpu_custom_call" | custom-call | tf_op jit(solution)/shard_map/pallas_call | solution.py:465
  300.3 1.9 copy.23
  302.2 1.5 copy.24
  303.7 1.5 copy.25
  (2 shorter events, 0.0 us)
Async XLA Ops:
  17.6 7.7 %copy-start = (bf16[2,256,512]{2,1,0:T(8,128)(2,1)S(1)}, bf16[2,256,512]{2,1,0:T(8,128)(2,1)}, u32[]{:S(2)}) copy-start(bf16[2,256,512]{2,1,0:T(8,128)(2,1)} %param.9) | copy-start | bytes 1572868
  17.6 8.1 %copy-start.1 = (bf16[2,256,2,128]{3,2,1,0:T(2,128)(2,1)S(1)}, bf16[2,256,2,128]{3,2,1,0:T(2,128)(2,1)}, u32[]{:S(2)}) copy-start(bf16[2,256,2,128]{3,2,1,0:T(2,128)(2,1)} %param.10) | copy-start | bytes 786436
  25.3 1.4 copy-start.2

commit v3 on v2

--- a/solution.py
+++ b/solution.py
@@ -2,6 +2,7 @@
 
 import jax
 import jax.numpy as jnp
+import numpy as np
 from jax import lax
 from jax.experimental import pallas as pl
 from jax.experimental.pallas import tpu as pltpu
@@ -19,22 +20,24 @@
 
 
 def rope_tables(seq_len, head_dim):
-    half_dim = head_dim // 2
-    inv_freq = ROPE_BASE ** (-2.0 * jnp.arange(half_dim, dtype=F32) / head_dim)
-    angles = jnp.arange(seq_len, dtype=F32)[:, None] * inv_freq[None, :]
-    return jnp.cos(angles), jnp.sin(angles)
-
-
-def layers_kernel(dims, x_ref, gamma_ref, cos_ref, sin_ref, wqkv, wgu, wo, wd,
+    inv_freq = np.float32(ROPE_BASE) ** (-2.0 * np.arange(head_dim // 2, dtype=np.float32) / head_dim).astype(np.float32)
+    angles = np.arange(seq_len, dtype=np.float32)[:, None] * inv_freq[None, :]
+    cos_tab, sin_tab = np.cos(angles.astype(np.float64)), np.sin(angles.astype(np.float64))
+    return (np.concatenate([cos_tab, cos_tab], axis=-1).astype(np.float32),
+            np.concatenate([-sin_tab, sin_tab], axis=-1).astype(np.float32))
+
+
+def layers_kernel(dims, gamma_ref, cos_ref, sin_ref, x_ref, wq, wkv, wgu, wo, wd,
                   y_out, k_out, v_out,
                   bqkv, bgu, bo, bd, hbuf, qbuf, kvbuf, obuf, mbuf, part, rs0, rs1, rs2, resid,
+                  gu_raw, kv_raw, gu_stage, kv_stage, raw_sem,
                   w_send, w_recv, a_send, a_recv, kv_send, kv_recv, r_send, r_recv, out_sem):
     layers, n_x, n_y, seq, head_dim, rows, width = dims
     heads = wo.shape[1] // CORES // head_dim
     hid = wd.shape[1] // CORES
     o_rows = wo.shape[1] // CORES
     q_cols = heads * head_dim
-    g_cols = wgu.shape[-1] // 2
+    g_cols = hid // GU_CHUNKS
     n_prompts = CORES * n_y
     toks = n_prompts * seq
     keep = n_y * seq
@@ -51,6 +54,27 @@
     def at_x(chip, core):
         return {'wx': chip * CORES + core}
 
+    n_gu = layers * GU_CHUNKS
+
+    def gu_load(g, core):
+        cols = pl.ds(core * hid + (g % GU_CHUNKS) * g_cols, g_cols)
+        return pltpu.make_async_copy(wgu.at[g // GU_CHUNKS, :, :, cols], gu_raw.at[g % 2, core], raw_sem.at[g % 2, core])
+
+    def kv_load(l):
+        return pltpu.make_async_copy(wkv.at[l], kv_raw.at[l], raw_sem.at[2, l])
+
+    def x_load(i):
+        return pltpu.make_async_copy(x_ref.at[0, :, pl.ds(i * width, width)], resid.at[i], raw_sem.at[3 + i // 2, i % 2])
+
+    kv_load(0).start()
+    for g in range(2):
+        for core in range(CORES):
+            gu_load(g, core).start()
+    for i in range(resid.shape[0]):
+        x_load(i).start()
+    for l in range(1, layers):
+        kv_load(l).start()
+
     barrier = pltpu.get_barrier_semaphore()
     peers = [sibling, right_y, left_y] + [at_x(chip, core) for chip in (xr, xl) for core in range(CORES)]
     for peer in peers:
@@ -70,8 +94,8 @@
     pieces = []
     n_blocks = 0
     for l in range(layers):
-        pieces.append([('qkv', l, 0, n_blocks)])
-        n_blocks += 1
+        pieces.append([('q', l, 0, n_blocks), ('kv', l, 0, n_blocks + 1)])
+        n_blocks += 2
         for j in range(GU_CHUNKS):
             pieces.append([('gu', l, j, n_blocks)])
             n_blocks += 1
@@ -79,13 +103,20 @@
             pieces.append([('o', l, hh, n_blocks), ('d', l, hh, n_blocks + 1)])
             n_blocks += 2
     per_layer = len(pieces) // layers
+    issue_after = [[p + 2] for p in range(len(pieces))]
+    tail = len(pieces) - HALVES
+    issue_after[tail - 2] = []
+    issue_after[tail - 1] = [tail + hh for hh in range(HALVES)]
+    issue_after[tail:] = [[] for _ in range(HALVES)]
 
     def source(block, core):
         kind, l, j, _ = block
-        if kind == 'qkv':
-            return wqkv.at[l, core]
+        if kind == 'q':
+            return wq.at[l, :, pl.ds(pl.multiple_of(core * q_cols, q_cols), q_cols)]
+        if kind == 'kv':
+            return kv_stage.at[l, core]
         if kind == 'gu':
-            return wgu.at[l, core, j]
+            return gu_stage.at[l, j, core]
         if kind == 'o':
             return wo.at[l, pl.ds(pl.multiple_of(core * o_rows, o_rows), o_rows), pl.ds(j * width, width)]
         return wd.at[l, pl.ds(pl.multiple_of(core * hid, hid), hid), pl.ds(j * width, width)]
@@ -94,18 +125,43 @@
         kind, l, j, _ = block
         row = pl.ds(pl.multiple_of((chip * CORES + core) * rows, rows), rows)
         col = pl.ds(pl.multiple_of(core * width, width), width)
-        if kind == 'qkv':
-            return bqkv.at[l, row]
+        if kind == 'q':
+            return bqkv.at[l, row, pl.ds(0, q_cols)]
+        if kind == 'kv':
+            return bqkv.at[l, row, pl.ds(q_cols, head_dim)]
         if kind == 'gu':
             return bgu.at[l, j, row]
         if kind == 'o':
             return bo.at[l, j, chip, :, col]
         return bd.at[l, j, chip, :, col]
 
-    def issue_own(p):
+    def prepare_kv(l):
+        kv_load(l).wait()
+        for core in range(CORES):
+            kv_stage[l, core] = kv_raw[l, :, core, :]
+
+    def prepare(p):
+        if p >= len(pieces) or pieces[p][0][0] != 'gu':
+            return
+        _, l, j, _ = pieces[p][0]
+        g = l * GU_CHUNKS + j
+        step_rows = rows // 4
+        for core in range(CORES):
+            gu_load(g, core).wait()
+
+            def step(i, carry):
+                at = pl.ds(pl.multiple_of(i * step_rows, step_rows), step_rows)
+                for which in range(2):
+                    gu_stage[l, j, core, at, which * g_cols:(which + 1) * g_cols] = gu_raw[g % 2, core, at, which, :]
+                return carry
+            lax.fori_loop(0, 4, step, 0)
+            if g + 2 < n_gu:
+                gu_load(g + 2, core).start()
+
+    def issue_own(p, only=None):
         if p >= len(pieces):
             return
-        for block in pieces[p]:
+        for block in pieces[p] if only is None else [pieces[p][only]]:
             t = block[3]
             here = landing(block, x, c)
             for core in range(CORES):
@@ -137,7 +193,9 @@
             wait_block(block, R1)
             from_right = landing(block, xr, 1)
             remote(from_right, from_right, w_send.at[t, 7], w_recv.at[t, FR], at_x(xl, c)).start()
-        issue_own(p + 2)
+        for later in issue_after[p]:
+            issue_own(later)
+        prepare(p + 3)
 
     def wait_piece(p, hows):
         for block in pieces[p]:
@@ -209,12 +267,14 @@
         scale = lax.rsqrt(square / d_model + LN_EPS)
         own = pl.ds(pl.multiple_of(y * seq, seq), seq)
         for i in range(n_res):
-            value = (resid[i].astype(F32) - mean) * scale * gamma_ref[l, i]
+            value = (resid[i].astype(F32) - mean) * scale * gamma_ref[l:l + 1, i * width:(i + 1) * width]
             hbuf[own, i * width:(i + 1) * width] = value.astype(BF)
 
     def rotate(value):
         value = value.astype(F32)
-        return (value * cos_ref[...] + pltpu.roll(value, head_dim // 2, 1) * sin_ref[...]).astype(BF)
+        cos_all = jnp.concatenate([cos_ref[...]] * (tile // seq), axis=0)
+        sin_all = jnp.concatenate([sin_ref[...]] * (tile // seq), axis=0)
+        return (value * cos_all + pltpu.roll(value, head_dim // 2, 1) * sin_all).astype(BF)
 
     def tiles(body, n=4, size=tile):
         def step(i, carry):
@@ -343,10 +403,15 @@
                 wait_out(rs1.at[k, side], r_recv.at[k, 1 + side], r_send.at[k, 1 + side])
                 wait_out(rs2.at[k, side], r_recv.at[k, 3 + side], r_send.at[k, 3 + side])
 
-    issue_own(0)
+    issue_own(0, 0)
+    for l in range(layers):
+        prepare_kv(l)
+    prepare(1)
+    issue_own(0, 1)
     issue_own(1)
+    prepare(2)
     for i in range(n_res):
-        resid[i] = x_ref[0, :, i * width:(i + 1) * width]
+        x_load(i).wait()
     norm_own(0)
     gather_send(0)
     comm(0)
@@ -373,7 +438,7 @@
         kv_finish(l)
         attend()
         for j in range(1, GU_CHUNKS):
-            ahead(base + 2 + j)
+            ahead(base + 1 + j if last and j == GU_CHUNKS - 1 else base + 2 + j)
             wait_piece(base + 1 + j, rest)
             gate_up(l, j)
         gather_drain(l)
@@ -384,13 +449,14 @@
         wait_piece(c1, (LOCAL, SIB))
         project_out(l, OWN, 1)
         reduce_cores(OWN, 0)
+        reduce_cores(OWN, 1)
+        reduce_far(OWN, 0)
+        ahead(c0)
         wait_piece(c0, (L1, R0))
         project_out(l, LEFT, 0)
-        reduce_cores(OWN, 1)
-        reduce_far(OWN, 0)
+        reduce_far(OWN, 1)
         project_out(l, RIGHT, 0)
         reduce_cores(LEFT, 0)
-        reduce_far(OWN, 1)
         reduce_cores(RIGHT, 0)
         reduce_last(l, OWN, 0)
         reduce_far(LEFT, 0)
@@ -435,6 +501,19 @@
                 out_copy((chips[b] * CORES + core) * HALVES + hh, chunk(b, hh), core).wait()
 
 
+def take_over(*refs):
+    sources, targets, held, sems = refs[:3], refs[3:6], refs[6:9], refs[9]
+    loads = [pltpu.make_async_copy(sources[n], held[n], sems.at[0, n]) for n in range(3)]
+    stores = [pltpu.make_async_copy(held[n], targets[n], sems.at[1, n]) for n in range(3)]
+    for load in loads:
+        load.start()
+    for n in (1, 2, 0):
+        loads[n].wait()
+        stores[n].start()
+    for store in stores:
+        store.wait()
+
+
 def run_layers(mesh_sizes, x_tokens, gamma_ln, w_q, w_kv, w_gu, w_o, w_d):
     n_x, n_y = mesh_sizes['wx'] // CORES, mesh_sizes['wy']
     assert n_x == 4 and n_y == 4 and x_tokens.shape[0] == 1
@@ -449,23 +528,15 @@
     toks = CORES * n_y * seq
     n_chunks = n_x * HALVES
     n_res = d_model // width
-    q_split = jnp.swapaxes(w_q.reshape(layers, rows, CORES, q_cols), 1, 2)
-    wqkv = jnp.concatenate([q_split, jnp.swapaxes(w_kv, 1, 2)], axis=-1)
-    wgu = w_gu.reshape(layers, rows, 2, CORES, GU_CHUNKS, g_cols).transpose(0, 3, 4, 1, 2, 5)
-    wgu = wgu.reshape(layers, CORES, GU_CHUNKS, rows, 2 * g_cols)
-    cos_tab, sin_tab = rope_tables(seq, head_dim)
-    reps = toks // 4 // seq
-    cos_all = jnp.tile(jnp.concatenate([cos_tab, cos_tab], axis=-1), (reps, 1))
-    sin_all = jnp.tile(jnp.concatenate([-sin_tab, sin_tab], axis=-1), (reps, 1))
-    gamma = gamma_ln.reshape(layers, n_res, 1, width)
-    blocks = layers * (1 + GU_CHUNKS + 2 * HALVES)
+    cos_all, sin_all = rope_tables(seq, head_dim)
+    blocks = layers * (2 + GU_CHUNKS + 2 * HALVES)
     dma = pltpu.SemaphoreType.DMA
     in_vmem, anywhere = pl.BlockSpec(memory_space=pltpu.VMEM), pl.BlockSpec(memory_space=pl.ANY)
     cache = jax.ShapeDtypeStruct((layers, 1, seq, head_dim), BF)
-    return pl.pallas_call(
+    results = pl.pallas_call(
         functools.partial(layers_kernel, (layers, n_x, n_y, seq, head_dim, rows, width)),
         out_shape=(jax.ShapeDtypeStruct(x_tokens.shape, BF), cache, cache),
-        in_specs=[in_vmem] * 4 + [anywhere] * 4,
+        in_specs=[in_vmem] * 3 + [anywhere] * 6,
         out_specs=(anywhere,) * 3,
         scratch_shapes=[
             pltpu.VMEM((layers, d_model, q_cols + head_dim), BF),
@@ -482,6 +553,11 @@
             pltpu.VMEM((n_chunks, 2, seq, width), F32),
             pltpu.VMEM((n_chunks, 2, seq, CORES * width), F32),
             pltpu.VMEM((n_res, seq, width), BF),
+            pltpu.VMEM((2, CORES, rows, 2, g_cols), BF),
+            pltpu.VMEM((layers, rows, 2, head_dim), BF),
+            pltpu.VMEM((layers, GU_CHUNKS, CORES, rows, 2 * g_cols), BF),
+            pltpu.VMEM((layers, 2, rows, head_dim), BF),
+            dma((3 + n_res // 2, 2)),
             dma((blocks, 8)), dma((blocks, 8)),
             dma((layers, 9)), dma((layers, 9)),
             dma((layers, 2)), dma((layers, 2)),
@@ -489,7 +565,12 @@
             dma((2 * layers + CORES * n_chunks,)),
         ],
         compiler_params=pltpu.CompilerParams(collective_id=0, has_side_effects=True, vmem_limit_bytes=67043328),
-    )(x_tokens, gamma, cos_all, sin_all, wqkv, wgu, w_o, w_d)
+    )(gamma_ln, cos_all, sin_all, x_tokens, w_q, w_kv, w_gu, w_o, w_d)
+    shapes = [jax.ShapeDtypeStruct(r.shape, r.dtype) for r in results]
+    return pl.pallas_call(
+        take_over, out_shape=shapes, in_specs=[anywhere] * 3, out_specs=[anywhere] * 3,
+        scratch_shapes=[pltpu.VMEM(r.shape, r.dtype) for r in results] + [dma((2, 3))],
+    )(*results)
 
 
 def solution(mesh):

time: 306 us -> 277 us (0.905)
  local copies, waits for them, and re-layouts: 30.2 us -> 0 us
    reshape x5 -> x0, local copies, waits for them, and re-layouts: 23.8 us -> none  [the longest x2 15.3 us: run_layers(): w_gu.reshape(layers, rows, 2, CORES, GU_CHUNKS, g_cols)]
    unnamed x11 -> x0, local copies, waits for them, and re-layouts: 5.08 us -> none
where the time goes in v3:
time: 277 us
  Pallas kernels  276 us (100%)
    pallas_call x1, Pallas kernels, run_layers(): pl.pallas_call(functools.partial(layers_kernel, (layers, n_x, n_y, seq, h...  274 us

profile of v3, /device:TPU:97, one launch (start us, length us, event | category | flops | bytes accessed | tf_op | source)
XLA Modules:
  0.0 276.7 jit_solution(15412002602436728102)
XLA Ops:
  0.6 274.0 %shard_map.112 = (bf16[1,128,2048]{2,1,0:T(8,128)(2,1)}, bf16[2,1,128,128]{3,2,1,0:T(8,128)(2,1)}, bf16[2,1,128,128]{3,2,1,0:T(8,128)(2,1)}) custom-call(f32[2,2048]{1,0:T(2,128)} %gamma_ref.1, f32[128,128]{1,0:T(8,128)} %constant.4.clone.cos_ref, f32[128,128]{1,0:T(8,128)} %constant.5.clone.sin_ref, bf16[1,128,2048]{2,1,0:T(8,128)(2,1)} %x_ref.1, ...), custom_call_target="tpu_custom_call" | custom-call | tf_op jit(solution)/shard_map/pallas_call | solution.py:536
  274.7 1.9 shard_map.113

commit v4 on v3

--- a/solution.py
+++ b/solution.py
@@ -15,8 +15,8 @@
 HALVES = 2
 BF, F32 = jnp.bfloat16, jnp.float32
 
-LOCAL, SIB, L0, L1, R0, R1, FL, FR = range(8)
-A_SIB, A_L, A_R, A_TOP, A_BOT, A_SL, A_SR, A_STOP, A_SBOT = range(9)
+L0, R1, SIDES, OWN_CHIP, FAR_CHIP = range(5)
+A_L, A_R, A_TOP, A_BOT, A_SIB = range(5)
 
 
 def rope_tables(seq_len, head_dim):
@@ -29,9 +29,9 @@
 
 def layers_kernel(dims, gamma_ref, cos_ref, sin_ref, x_ref, wq, wkv, wgu, wo, wd,
                   y_out, k_out, v_out,
-                  bqkv, bgu, bo, bd, hbuf, qbuf, kvbuf, obuf, mbuf, part, rs0, rs1, rs2, resid,
+                  bq, bkv, bgu, bo, bd, hbuf, qbuf, kvbuf, obuf, mbuf, part, rs0, rs1, rs2, resid,
                   gu_raw, kv_raw, gu_stage, kv_stage, raw_sem,
-                  w_send, w_recv, a_send, a_recv, kv_send, kv_recv, r_send, r_recv, out_sem):
+                  w_send, w_recv, kvw_send, kvw_recv, a_send, a_recv, kv_send, kv_recv, r_send, r_recv, out_sem):
     layers, n_x, n_y, seq, head_dim, rows, width = dims
     heads = wo.shape[1] // CORES // head_dim
     hid = wd.shape[1] // CORES
@@ -55,16 +55,18 @@
         return {'wx': chip * CORES + core}
 
     n_gu = layers * GU_CHUNKS
+    kv_rows = rows // n_y
 
     def gu_load(g, core):
         cols = pl.ds(core * hid + (g % GU_CHUNKS) * g_cols, g_cols)
-        return pltpu.make_async_copy(wgu.at[g // GU_CHUNKS, :, :, cols], gu_raw.at[g % 2, core], raw_sem.at[g % 2, core])
+        return pltpu.make_async_copy(wgu.at[g // GU_CHUNKS, :, :, cols], gu_raw.at[g % 2, core], raw_sem.at[g % 2])
 
     def kv_load(l):
-        return pltpu.make_async_copy(wkv.at[l], kv_raw.at[l], raw_sem.at[2, l])
+        mine = pl.ds(pl.multiple_of(y * kv_rows, kv_rows), kv_rows)
+        return pltpu.make_async_copy(wkv.at[l, mine], kv_raw.at[l], raw_sem.at[3 + l])
 
     def x_load(i):
-        return pltpu.make_async_copy(x_ref.at[0, :, pl.ds(i * width, width)], resid.at[i], raw_sem.at[3 + i // 2, i % 2])
+        return pltpu.make_async_copy(x_ref.at[0, :, pl.ds(i * width, width)], resid.at[i], raw_sem.at[2])
 
     kv_load(0).start()
     for g in range(2):
@@ -91,6 +93,7 @@
     def wait_out(ref, recv_sem, send_sem):
         remote(ref, ref, send_sem, recv_sem, sibling).wait_send()
 
+    order = ('q', 'kv', 'gu', 'o', 'd')
     pieces = []
     n_blocks = 0
     for l in range(layers):
@@ -126,9 +129,9 @@
         row = pl.ds(pl.multiple_of((chip * CORES + core) * rows, rows), rows)
         col = pl.ds(pl.multiple_of(core * width, width), width)
         if kind == 'q':
-            return bqkv.at[l, row, pl.ds(0, q_cols)]
+            return bq.at[l, row]
         if kind == 'kv':
-            return bqkv.at[l, row, pl.ds(q_cols, head_dim)]
+            return bkv.at[l, chip * CORES + core, y]
         if kind == 'gu':
             return bgu.at[l, j, row]
         if kind == 'o':
@@ -146,9 +149,8 @@
         _, l, j, _ = pieces[p][0]
         g = l * GU_CHUNKS + j
         step_rows = rows // 4
+        pltpu.make_async_copy(gu_raw.at[g % 2], gu_raw.at[g % 2], raw_sem.at[g % 2]).wait()
         for core in range(CORES):
-            gu_load(g, core).wait()
-
             def step(i, carry):
                 at = pl.ds(pl.multiple_of(i * step_rows, step_rows), step_rows)
                 for which in range(2):
@@ -164,19 +166,29 @@
         for block in pieces[p] if only is None else [pieces[p][only]]:
             t = block[3]
             here = landing(block, x, c)
+            sent = w_send.at[order.index(block[0])]
+            side = [SIDES * c, SIDES - c]
             for core in range(CORES):
-                remote(source(block, core), here, w_send.at[t, 2 + core], w_recv.at[t, L0 + c], at_x(xr, core)).start()
-                remote(source(block, core), here, w_send.at[t, 4 + core], w_recv.at[t, R0 + c], at_x(xl, core)).start()
-            remote(source(block, 1 - c), here, w_send.at[t, SIB], w_recv.at[t, SIB], sibling).start()
-            pltpu.make_async_copy(source(block, c), here, w_recv.at[t, LOCAL]).start()
+                remote(source(block, core), here, sent, w_recv.at[t, side[0]], at_x(xr, core)).start()
+                remote(source(block, core), here, sent, w_recv.at[t, side[1]], at_x(xl, core)).start()
+            remote(source(block, 1 - c), here, sent, w_recv.at[t, OWN_CHIP], sibling).start()
+            pltpu.make_async_copy(source(block, c), here, w_recv.at[t, OWN_CHIP]).start()
+
+    def pair(block, chip):
+        kind, l, j, _ = block
+        row = pl.ds(pl.multiple_of(chip * CORES * rows, CORES * rows), CORES * rows)
+        if kind == 'q':
+            return bq.at[l, row]
+        if kind == 'kv':
+            return bkv.at[l, pl.ds(chip * CORES, CORES), y]
+        if kind == 'gu':
+            return bgu.at[l, j, row]
+        return (bo if kind == 'o' else bd).at[l, j, chip]
 
     def wait_block(block, how):
-        t = block[3]
-        if how == LOCAL:
-            pltpu.make_async_copy(source(block, c), landing(block, x, c), w_recv.at[t, LOCAL]).wait()
-            return
-        chip, core = {SIB: (x, 1 - c), L0: (xl, 0), L1: (xl, 1), R0: (xr, 0), R1: (xr, 1), FL: (xo, 0), FR: (xo, 1)}[how]
-        wait_in(landing(block, chip, core), w_recv.at[t, how], w_send.at[t, 0])
+        ref = {L0: lambda: landing(block, xl, 0), R1: lambda: landing(block, xr, 1), SIDES: lambda: pair(block, xl),
+               OWN_CHIP: lambda: pair(block, x), FAR_CHIP: lambda: pair(block, xo)}[how]()
+        wait_in(ref, w_recv.at[block[3], how], w_send.at[0])
 
     done = [0]
 
@@ -189,10 +201,10 @@
             t = block[3]
             wait_block(block, L0)
             from_left = landing(block, xl, 0)
-            remote(from_left, from_left, w_send.at[t, 6], w_recv.at[t, FL], at_x(xr, c)).start()
+            remote(from_left, from_left, w_send.at[order.index(block[0])], w_recv.at[t, FAR_CHIP], at_x(xr, c)).start()
             wait_block(block, R1)
             from_right = landing(block, xr, 1)
-            remote(from_right, from_right, w_send.at[t, 7], w_recv.at[t, FR], at_x(xl, c)).start()
+            remote(from_right, from_right, w_send.at[order.index(block[0])], w_recv.at[t, FAR_CHIP], at_x(xl, c)).start()
         for later in issue_after[p]:
             issue_own(later)
         prepare(p + 3)
@@ -203,10 +215,34 @@
                 wait_block(block, how)
 
     def drain_weights():
-        for piece in pieces:
-            for block in piece:
-                for kind in range(1, 8):
-                    wait_out(landing(block, x, c), w_recv.at[block[3], SIB], w_send.at[block[3], kind])
+        sources = n_x * CORES
+        for n, ref in enumerate((bq.at[:, pl.ds(0, (sources - 1) * rows)], bkv.at[:, pl.ds(0, sources - 1), 0],
+                                 bgu.at[:, :, pl.ds(0, (sources - 1) * rows)],
+                                 bo.at[:, :, :, pl.ds(0, o_rows // sources * (sources - 1))],
+                                 bd.at[:, :, :, pl.ds(0, hid // sources * (sources - 1))])):
+            wait_out(ref, w_recv.at[0, 0], w_send.at[n])
+
+    def kv_quarter(l, yy, half=None):
+        n_src = n_x * CORES
+        return bkv.at[l, pl.ds(0 if half is None else half * (n_src // 2), n_src if half is None else n_src // 2), yy]
+
+    def kvw_copy(l, ref, kind, peer):
+        remote(ref, ref, kvw_send.at[l], kvw_recv.at[l, kind], peer).start()
+
+    def kvw_send_own(l):
+        kvw_copy(l, kv_quarter(l, y), A_L, right_y)
+        kvw_copy(l, kv_quarter(l, y), A_R, left_y)
+
+    def kvw_forward(l):
+        wait_in(kv_quarter(l, yl), kvw_recv.at[l, A_L], kvw_send.at[l])
+        kvw_copy(l, kv_quarter(l, yl, 0), A_TOP, right_y)
+        wait_in(kv_quarter(l, yr), kvw_recv.at[l, A_R], kvw_send.at[l])
+        kvw_copy(l, kv_quarter(l, yr, 1), A_BOT, left_y)
+
+    def kvw_finish(l):
+        wait_in(kv_quarter(l, yo, 0), kvw_recv.at[l, A_TOP], kvw_send.at[l])
+        wait_in(kv_quarter(l, yo, 1), kvw_recv.at[l, A_BOT], kvw_send.at[l])
+        wait_out(bkv.at[l, :, pl.ds(0, n_y - 1)], kvw_recv.at[l, A_L], kvw_send.at[l])
 
     def prompt(slot, part_of=None):
         if part_of is None:
@@ -215,10 +251,10 @@
         return hbuf.at[pl.ds(pl.multiple_of(slot * seq + part_of * half, half), half)]
 
     def a_copy(l, src, dst, kind, peer):
-        remote(src, dst, a_send.at[l, kind], a_recv.at[l, kind], peer).start()
+        remote(src, dst, a_send.at[l], a_recv.at[l, kind], peer).start()
 
     def a_wait(l, ref, kind):
-        wait_in(ref, a_recv.at[l, kind], a_send.at[l, kind])
+        wait_in(ref, a_recv.at[l, kind], a_send.at[l])
 
     def gather_send(l):
         a_copy(l, prompt(y), prompt(y), A_L, right_y)
@@ -228,29 +264,22 @@
     def gather_forward(l):
         a_wait(l, prompt(yl), A_L)
         a_copy(l, prompt(yl, 0), prompt(yl, 0), A_TOP, right_y)
-        a_copy(l, prompt(yl), prompt(n_y + yl), A_SL, sibling)
+        a_copy(l, prompt(yl), prompt(n_y + yl), A_SIB, sibling)
         a_wait(l, prompt(yr), A_R)
         a_copy(l, prompt(yr, 1), prompt(yr, 1), A_BOT, left_y)
-        a_copy(l, prompt(yr), prompt(n_y + yr), A_SR, sibling)
+        a_copy(l, prompt(yr), prompt(n_y + yr), A_SIB, sibling)
 
     def gather_share(l):
         a_wait(l, prompt(yo, 0), A_TOP)
-        a_copy(l, prompt(yo, 0), prompt(n_y + yo, 0), A_STOP, sibling)
+        a_copy(l, prompt(yo, 0), prompt(n_y + yo, 0), A_SIB, sibling)
         a_wait(l, prompt(yo, 1), A_BOT)
-        a_copy(l, prompt(yo, 1), prompt(n_y + yo, 1), A_SBOT, sibling)
+        a_copy(l, prompt(yo, 1), prompt(n_y + yo, 1), A_SIB, sibling)
 
     def gather_finish(l):
-        a_wait(l, prompt(n_y + y), A_SIB)
-        a_wait(l, prompt(n_y + yl), A_SL)
-        a_wait(l, prompt(n_y + yr), A_SR)
-        a_wait(l, prompt(n_y + yo, 0), A_STOP)
-        a_wait(l, prompt(n_y + yo, 1), A_SBOT)
+        a_wait(l, hbuf.at[pl.ds(keep, keep)], A_SIB)
 
     def gather_drain(l):
-        for kind in (A_L, A_R, A_SIB, A_SL, A_SR):
-            wait_out(prompt(y), a_recv.at[l, kind], a_send.at[l, kind])
-        for kind in (A_TOP, A_BOT, A_STOP, A_SBOT):
-            wait_out(prompt(y, 0), a_recv.at[l, kind], a_send.at[l, kind])
+        wait_out(hbuf.at[pl.ds(0, 7 * seq)], a_recv.at[l, A_L], a_send.at[l])
 
     n_res = resid.shape[0]
     d_model = n_res * width
@@ -282,13 +311,19 @@
             return carry
         lax.fori_loop(0, n, step, 0)
 
-    def project_qkv(l):
+    def project_q(l):
         def body(start):
             at = pl.ds(start, tile)
-            acc = jnp.dot(hbuf[at, :], bqkv[l], preferred_element_type=F32).astype(BF)
+            acc = jnp.dot(hbuf[at, :], bq[l], preferred_element_type=F32).astype(BF)
             for n in range(heads):
                 qbuf[at, n * head_dim:(n + 1) * head_dim] = rotate(acc[:, n * head_dim:(n + 1) * head_dim])
-            kv = acc[:, q_cols:]
+        tiles(body)
+
+    def project_kv(l):
+        def body(start):
+            at = pl.ds(start, tile)
+            weights = bkv[l].reshape(d_model, head_dim)
+            kv = jnp.dot(hbuf[at, :], weights, preferred_element_type=F32).astype(BF)
             kvbuf[c, at, :] = jnp.where(c == 0, rotate(kv), kv)
         tiles(body)
 
@@ -297,24 +332,22 @@
 
     def kv_exchange(l):
         for lo in range(2):
-            remote(kv_refs(lo), kv_refs(1 - lo), kv_send.at[l, lo], kv_recv.at[l, lo], sibling).start()
+            remote(kv_refs(lo), kv_refs(1 - lo), kv_send.at[l], kv_recv.at[l], sibling).start()
 
     def kv_outs(l):
         own = pl.ds(pl.multiple_of(y * seq, seq), seq)
-        return [pltpu.make_async_copy(kvbuf.at[0, own], k_out.at[l, 0], out_sem.at[2 * l]),
-                pltpu.make_async_copy(kvbuf.at[1, own], v_out.at[l, 0], out_sem.at[2 * l + 1])]
+        return [pltpu.make_async_copy(kvbuf.at[0, own], k_out.at[l, 0], out_sem.at[l]),
+                pltpu.make_async_copy(kvbuf.at[1, own], v_out.at[l, 0], out_sem.at[l])]
 
     def kv_finish(l):
-        for lo in range(2):
-            wait_in(kvbuf.at[1 - c, pl.ds((1 - lo) * keep, keep)], kv_recv.at[l, lo], kv_send.at[l, lo])
+        wait_in(kvbuf.at[1 - c], kv_recv.at[l], kv_send.at[l])
         for copy in kv_outs(l):
             copy.start()
 
     def kv_drain(l):
-        for lo in range(2):
-            wait_out(kv_refs(lo), kv_recv.at[l, lo], kv_send.at[l, lo])
-        for copy in kv_outs(l):
-            copy.wait()
+        wait_out(kvbuf.at[c], kv_recv.at[l], kv_send.at[l])
+        both = kvbuf.at[0, pl.ds(0, 2 * seq)]
+        pltpu.make_async_copy(both, both, out_sem.at[l]).wait()
 
     def attend():
         score_scale = head_dim ** -0.5
@@ -355,9 +388,12 @@
 
         def step(i, carry):
             body(pl.multiple_of(((i + 2) % 4) * tile, tile))
+
+            @pl.when(i == 1)
+            def _():
+                remote(part.at[k, pl.ds(keep, keep)], rs0.at[k], r_send.at[0], r_recv.at[k, 0], sibling).start()
             return carry
         lax.fori_loop(0, 4, step, 0)
-        remote(part.at[k, pl.ds(keep, keep)], rs0.at[k], r_send.at[k, 0], r_recv.at[k, 0], sibling).start()
 
     def of_chip(k, yy):
         return part.at[k, pl.ds(pl.multiple_of(yy * seq, seq), seq)]
@@ -367,41 +403,37 @@
 
     def reduce_cores(b, hh):
         k = chunk(b, hh)
-        wait_in(rs0.at[k], r_recv.at[k, 0], r_send.at[k, 0])
+        wait_in(rs0.at[k], r_recv.at[k, 0], r_send.at[0])
         part[k, 0:keep, :] += rs0[k]
-        remote(of_chip_half(k, yo, 0), rs1.at[k, 0], r_send.at[k, 1], r_recv.at[k, 1], right_y).start()
-        remote(of_chip_half(k, yo, 1), rs1.at[k, 1], r_send.at[k, 2], r_recv.at[k, 2], left_y).start()
+        remote(of_chip_half(k, yo, 0), rs1.at[k, 0], r_send.at[1], r_recv.at[k, 1], right_y).start()
+        remote(of_chip_half(k, yo, 1), rs1.at[k, 1], r_send.at[1], r_recv.at[k, 2], left_y).start()
 
     def reduce_far(b, hh):
         k = chunk(b, hh)
         for side, target, peer in ((0, yr, right_y), (1, yl, left_y)):
-            wait_in(rs1.at[k, side], r_recv.at[k, 1 + side], r_send.at[k, 1 + side])
+            wait_in(rs1.at[k, side], r_recv.at[k, 1 + side], r_send.at[1])
             at = pl.ds(pl.multiple_of(target * seq, seq), seq)
             part[k, at, side * half_w:(side + 1) * half_w] += rs1[k, side]
-            remote(of_chip(k, target), rs2.at[k, side], r_send.at[k, 3 + side], r_recv.at[k, 3 + side], peer).start()
-
-    def out_copy(i, k, core):
+            remote(of_chip(k, target), rs2.at[k, side], r_send.at[2], r_recv.at[k, 3], peer).start()
+
+    def out_copy(i):
         return pltpu.make_async_copy(resid.at[i], y_out.at[0, :, pl.ds(pl.multiple_of(i * width, width), width)],
-                                     out_sem.at[2 * layers + CORES * k + core])
+                                     out_sem.at[layers])
 
     def reduce_last(l, b, hh):
         k = chunk(b, hh)
-        for side in range(2):
-            wait_in(rs2.at[k, side], r_recv.at[k, 3 + side], r_send.at[k, 3 + side])
+        wait_in(rs2.at[k], r_recv.at[k, 3], r_send.at[2])
         own = pl.ds(pl.multiple_of(y * seq, seq), seq)
         total = part[k, own, :] + rs2[k, 0] + rs2[k, 1]
         for core in range(CORES):
             i = (chips[b] * CORES + core) * HALVES + hh
             resid[i] = (resid[i].astype(F32) + total[:, core * width:(core + 1) * width]).astype(BF)
             if l == layers - 1:
-                out_copy(i, k, core).start()
+                out_copy(i).start()
 
     def reduce_drain():
-        for k in range(len(chips) * HALVES):
-            wait_out(rs0.at[k], r_recv.at[k, 0], r_send.at[k, 0])
-            for side in range(2):
-                wait_out(rs1.at[k, side], r_recv.at[k, 1 + side], r_send.at[k, 1 + side])
-                wait_out(rs2.at[k, side], r_recv.at[k, 3 + side], r_send.at[k, 3 + side])
+        for n, ref in enumerate((rs0, rs1, rs2)):
+            wait_out(ref, r_recv.at[0, 0], r_send.at[n])
 
     issue_own(0, 0)
     for l in range(layers):
@@ -410,16 +442,15 @@
     issue_own(0, 1)
     issue_own(1)
     prepare(2)
-    for i in range(n_res):
-        x_load(i).wait()
+    pltpu.make_async_copy(resid, resid, raw_sem.at[2]).wait()
     norm_own(0)
     gather_send(0)
     comm(0)
     gather_forward(0)
     gather_share(0)
     gather_finish(0)
-    rest = (LOCAL, SIB, L1, R0, FL, FR)
     OWN, LEFT, RIGHT, FAR = range(4)
+    rest = (OWN_CHIP, SIDES, FAR_CHIP)
     for l in range(layers):
         base = l * per_layer
         last = l == layers - 1
@@ -430,29 +461,34 @@
 
         ahead(base + 1)
         wait_piece(base, rest)
-        project_qkv(l)
-        kv_exchange(l)
+        kvw_send_own(l)
+        project_q(l)
         ahead(base + 2)
+        kvw_forward(l)
         wait_piece(base + 1, rest)
         gate_up(l, 0)
-        kv_finish(l)
-        attend()
+        kvw_finish(l)
+        project_kv(l)
+        kv_exchange(l)
         for j in range(1, GU_CHUNKS):
             ahead(base + 1 + j if last and j == GU_CHUNKS - 1 else base + 2 + j)
             wait_piece(base + 1 + j, rest)
             gate_up(l, j)
+            if j == 1:
+                kv_finish(l)
+                attend()
         gather_drain(l)
         kv_drain(l)
         c0, c1 = base + 1 + GU_CHUNKS, base + 2 + GU_CHUNKS
-        wait_piece(c0, (LOCAL, SIB))
+        wait_piece(c0, (OWN_CHIP,))
         project_out(l, OWN, 0)
-        wait_piece(c1, (LOCAL, SIB))
+        wait_piece(c1, (OWN_CHIP,))
         project_out(l, OWN, 1)
         reduce_cores(OWN, 0)
         reduce_cores(OWN, 1)
         reduce_far(OWN, 0)
         ahead(c0)
-        wait_piece(c0, (L1, R0))
+        wait_piece(c0, (SIDES,))
         project_out(l, LEFT, 0)
         reduce_far(OWN, 1)
         project_out(l, RIGHT, 0)
@@ -461,27 +497,27 @@
         reduce_last(l, OWN, 0)
         reduce_far(LEFT, 0)
         comm(c1)
-        wait_piece(c1, (L1, R0))
+        wait_piece(c1, (SIDES,))
         project_out(l, LEFT, 1)
         reduce_far(RIGHT, 0)
         reduce_last(l, OWN, 1)
         project_out(l, RIGHT, 1)
         reduce_cores(LEFT, 1)
-        wait_piece(c0, (FL, FR))
+        reduce_cores(RIGHT, 1)
+        wait_piece(c0, (FAR_CHIP,))
         project_out(l, FAR, 0)
-        reduce_cores(RIGHT, 1)
         reduce_last(l, LEFT, 0)
         reduce_far(LEFT, 1)
+        reduce_far(RIGHT, 1)
+        reduce_cores(FAR, 0)
         if not last:
             comm(c1 + 1)
-        wait_piece(c1, (FL, FR))
+        reduce_far(FAR, 0)
+        wait_piece(c1, (FAR_CHIP,))
         project_out(l, FAR, 1)
-        reduce_cores(FAR, 0)
         reduce_last(l, RIGHT, 0)
-        reduce_far(RIGHT, 1)
         reduce_cores(FAR, 1)
         reduce_last(l, LEFT, 1)
-        reduce_far(FAR, 0)
         reduce_last(l, RIGHT, 1)
         reduce_far(FAR, 1)
         reduce_last(l, FAR, 0)
@@ -495,10 +531,7 @@
             gather_share(l + 1)
             gather_finish(l + 1)
     drain_weights()
-    for b in range(len(chips)):
-        for hh in range(HALVES):
-            for core in range(CORES):
-                out_copy((chips[b] * CORES + core) * HALVES + hh, chunk(b, hh), core).wait()
+    pltpu.make_async_copy(resid, resid, out_sem.at[layers]).wait()
 
 
 def take_over(*refs):
@@ -539,7 +572,8 @@
         in_specs=[in_vmem] * 3 + [anywhere] * 6,
         out_specs=(anywhere,) * 3,
         scratch_shapes=[
-            pltpu.VMEM((layers, d_model, q_cols + head_dim), BF),
+            pltpu.VMEM((layers, d_model, q_cols), BF),
+            pltpu.VMEM((layers, n_x * CORES, n_y, rows // n_y, head_dim), BF),
             pltpu.VMEM((layers, GU_CHUNKS, d_model, 2 * g_cols), BF),
             pltpu.VMEM((layers, HALVES, n_x, q_cols, CORES * width), BF),
             pltpu.VMEM((layers, HALVES, n_x, hid, CORES * width), BF),
@@ -554,15 +588,16 @@
             pltpu.VMEM((n_chunks, 2, seq, CORES * width), F32),
             pltpu.VMEM((n_res, seq, width), BF),
             pltpu.VMEM((2, CORES, rows, 2, g_cols), BF),
-            pltpu.VMEM((layers, rows, 2, head_dim), BF),
+            pltpu.VMEM((layers, rows // n_y, 2, head_dim), BF),
             pltpu.VMEM((layers, GU_CHUNKS, CORES, rows, 2 * g_cols), BF),
-            pltpu.VMEM((layers, 2, rows, head_dim), BF),
-            dma((3 + n_res // 2, 2)),
-            dma((blocks, 8)), dma((blocks, 8)),
-            dma((layers, 9)), dma((layers, 9)),
-            dma((layers, 2)), dma((layers, 2)),
-            dma((n_chunks, 5)), dma((n_chunks, 5)),
-            dma((2 * layers + CORES * n_chunks,)),
+            pltpu.VMEM((layers, 2, rows // n_y, head_dim), BF),
+            dma((3 + layers,)),
+            dma((5,)), dma((blocks, 5)),
+            dma((layers,)), dma((layers, 4)),
+            dma((layers,)), dma((layers, 5)),
+            dma((layers,)), dma((layers,)),
+            dma((3,)), dma((n_chunks, 4)),
+            dma((layers + 1,)),
         ],
         compiler_params=pltpu.CompilerParams(collective_id=0, has_side_effects=True, vmem_limit_bytes=67043328),
     )(gamma_ln, cos_all, sin_all, x_tokens, w_q, w_kv, w_gu, w_o, w_d)

time: 277 us -> 267 us (0.964)
  Pallas kernels: 276 us -> 266 us
    pallas_call x1, Pallas kernels: 274 us -> 264 us  [run_layers(): pl.pallas_call(functools.partial(layers_kernel, (layers, n_x, n_y, seq, h...]
where the time goes in v4:
time: 267 us
  Pallas kernels  266 us (100%)
    pallas_call x1, Pallas kernels, run_layers(): pl.pallas_call(functools.partial(layers_kernel, (layers, n_x, n_y, seq, h...  264 us

profile of v4, /device:TPU:97, one launch (start us, length us, event | category | flops | bytes accessed | tf_op | source)
XLA Modules:
  0.0 267.1 jit_solution(8605569860720574204)
XLA Ops:
  0.6 264.4 %shard_map.112 = (bf16[1,128,2048]{2,1,0:T(8,128)(2,1)}, bf16[2,1,128,128]{3,2,1,0:T(8,128)(2,1)}, bf16[2,1,128,128]{3,2,1,0:T(8,128)(2,1)}) custom-call(f32[2,2048]{1,0:T(2,128)} %gamma_ref.1, f32[128,128]{1,0:T(8,128)} %constant.4.clone.cos_ref, f32[128,128]{1,0:T(8,128)} %constant.5.clone.sin_ref, bf16[1,128,2048]{2,1,0:T(8,128)(2,1)} %x_ref.1, ...), custom_call_target="tpu_custom_call" | custom-call | tf_op jit(solution)/shard_map/pallas_call | solution.py:569
  265.1 1.9 shard_map.113
